TPU v7x, 512 devices: a whole 4x8x8 slice. The times are simulated.
512 devices in a mesh: rows: 128 (over y, z, core), rep: 4 (over x).
Axes of the slice: x: 4, y: 8, z: 8, core: 2. Of those that a mesh axis runs over, the one named last changes fastest.
Arguments:
- embed: bfloat16 [65536, 1024], P('rows'), may hold values from -6 to 6
- start: bfloat16 [65536, 128], P('rows'), may hold values from -6 to 6
- links: int32 [128, 128], P('rows'), may hold values from -1 to 3, as said below
Outputs:
- embedding: float32 [65536, 128], P('rows')
Inputs may be any that keep to these rules, and one draw needn't show every extreme that they name: `links`: entry [r, s] is -1 (no pair) or a block of owner s; the diagonal is -1; each row has at most 96 entries other than -1, and some row has exactly 96.
All inputs are finite; a program needn't handle non-finite values.
Results may differ from a plain program's by a relative error of at most 0.012.
Values may be sent and summed in bfloat16 or wider, within the bound.
No kernel may reach another device: no remote copies, remote signals or barrier semaphores. Data moves between devices by JAX's collectives and lax.ppermute only.
A program may use at most 128 MiB of HBM per device.

v0:
```python
import functools
import math

import jax
import jax.numpy as jnp
from jax import lax
from jax.experimental import pallas as pl
from jax.experimental.pallas import tpu as pltpu
from jax.sharding import Mesh, PartitionSpec as P


BLOCK = 128
PAIR = 2 * BLOCK
EXTRA = 8
GROUP = 8
ITERS = 2
EPSILON = 1e-06
ROWS = ("y", "z", "c")
ROW_GROUP = ("z", "xb")
COL_GROUP = ("y", "c", "xa")


def from_everyone(shard, axes):
    copies = jnp.broadcast_to(shard, (lax.axis_size(axes), *shard.shape))
    return lax.all_to_all(copies, axes, split_axis=0, concat_axis=0, tiled=True)


def total_of(shard, axes):
    return jnp.sum(from_everyone(shard, axes), axis=0)


def gram_total(gram):
    wide = ("z", "xa", "xb")
    parts = gram.reshape(lax.axis_size(wide), -1, gram.shape[1])
    share = jnp.sum(lax.all_to_all(parts, wide, split_axis=0, concat_axis=0, tiled=True), axis=0)
    share = total_of(share, ("y", "c"))
    return from_everyone(share, wide).reshape(gram.shape)


def inverse_factor_kernel(gram_ref, out_ref):
    size = gram_ref.shape[0]
    count = size // GROUP
    diag = lax.broadcasted_iota(jnp.int32, (GROUP, size), 1) - lax.broadcasted_iota(
        jnp.int32, (GROUP, size), 0
    )
    sub = lax.broadcasted_iota(jnp.int32, (GROUP, size), 0)
    left = [gram_ref[g * GROUP : (g + 1) * GROUP] for g in range(count)]
    right = [(diag == g * GROUP).astype(jnp.float32) for g in range(count)]
    pivots = [None] * count

    def wide(column):
        return jnp.broadcast_to(column, (GROUP, size))

    def tall(row):
        return jnp.broadcast_to(row, (GROUP, size))

    for k in range(0, size, 2):
        home, at = divmod(k, GROUP)
        here = slice(at, at + 1)
        after = slice(at + 1, at + 2)
        first = [wide(left[g][:, k : k + 1]) for g in range(home, count)]
        second = [wide(left[g][:, k + 1 : k + 2]) for g in range(home, count)]
        a = tall(first[0][here])
        b = tall(first[0][after])
        d = tall(second[0][after])
        ratio = b / a
        rest = d - b * ratio
        inv_a, inv_rest = 1.0 / a, 1.0 / rest
        row_left, row_right = tall(left[home][here]), tall(right[home][here])
        next_left = tall(left[home][after]) - ratio * row_left
        next_right = tall(right[home][after]) - ratio * row_right
        for g in range(home, count):
            f = first[g - home] * inv_a
            h = (second[g - home] - first[g - home] * ratio) * inv_rest
            if g == home:
                mine = jnp.where(sub == at, a, jnp.where(sub == at + 1, rest, 0.0))
                pivots[g] = mine if pivots[g] is None else pivots[g] + mine
                f = jnp.where(sub > at, f, 0.0)
                h = jnp.where(sub > at + 1, h, 0.0)
            if g > home or at + 2 < GROUP:
                left[g] = left[g] - f * row_left - h * next_left
            right[g] = right[g] - f * row_right - h * next_right
    for g in range(count):
        out_ref[g * GROUP : (g + 1) * GROUP] = right[g] * lax.rsqrt(pivots[g])


def inverse_factor(gram):
    return pl.pallas_call(
        inverse_factor_kernel,
        out_shape=jax.ShapeDtypeStruct(gram.shape, jnp.float32),
        in_specs=[pl.BlockSpec(memory_space=pltpu.VMEM)],
        out_specs=pl.BlockSpec(memory_space=pltpu.VMEM),
        name="inverse_factor",
    )(gram)


def orthonormal(result, gram_matrix):
    inverse = inverse_factor(gram_matrix)
    return lax.dot_general(
        result, inverse, (((1,), (1,)), ((), ())), precision=lax.Precision.HIGHEST
    )


def exchange(row_own, col_own):
    size = lax.axis_size("z")
    assert size == lax.axis_size("y")
    onward = [(i, (i + 1) % size) for i in range(size)]
    backward = [(i, (i - 1) % size) for i in range(size)]
    height = row_own.shape[0]
    rows, cols = [], []

    def keep(place, first, piece):
        cols.append((piece, 0, place, first, False, piece.shape[0]))
        other = lax.ppermute(piece, "c", [(0, 1), (1, 0)])
        cols.append((other, 0, place, first, True, piece.shape[0]))

    rows.append((row_own, 0, 0, 0, height))
    keep(0, 0, col_own)
    row_a = row_b = row_own
    col_a = col_b = col_own
    for step in range(1, size // 2):
        col_a = lax.ppermute(col_a, "y", onward)
        col_b = lax.ppermute(col_b, "y", backward)
        row_a = lax.ppermute(row_a, "z", onward)
        row_b = lax.ppermute(row_b, "z", backward)
        rows.append((row_a, 0, size - step, 0, height))
        rows.append((row_b, 0, step, 0, height))
        keep(size - step, 0, col_a)
        keep(step, 0, col_b)
    far = size // 2
    col_top = lax.ppermute(col_a[:BLOCK], "y", onward)
    col_rest = lax.ppermute(col_b[BLOCK:], "y", backward)
    row_top = lax.ppermute(row_a[:BLOCK], "z", onward)
    row_rest = lax.ppermute(row_b[BLOCK:], "z", backward)
    rows.append((row_top, 0, far, 0, BLOCK))
    rows.append((row_rest, 0, far, BLOCK, height - BLOCK))
    keep(far, 0, col_top)
    keep(far, BLOCK, col_rest)
    return rows, cols


def tile_kernel(plan, sizes, ids, *refs):
    y_count, z_count, features, comps = sizes
    count, row_plan, col_plan = plan
    pieces, (w_out, sums_out, v_out) = refs[:count], refs[count : count + 3]
    rows_v, cols_v, start_v, row_links, col_links, weight, w_v, sems, out_sems = refs[count + 3 :]
    y, z, c, xa, xb = (ids[i] for i in range(5))
    row_owners, col_owners = z_count, 2 * y_count
    copies = []

    def copy(src, dst):
        made = pltpu.make_async_copy(src, dst, sems.at[len(copies)])
        made.start()
        copies.append(made)

    for slot, source, k, first, height in row_plan:
        ref = pieces[slot]
        owner = lax.rem(z + k, z_count)
        body = min(height, PAIR - first)
        at = pl.multiple_of(owner * PAIR + first, BLOCK)
        copy(ref.at[pl.ds(source, body)], rows_v.at[pl.ds(at, body)])
        if first + height > PAIR:
            copy(ref.at[pl.ds(source + body, EXTRA), pl.ds(0, BLOCK)], row_links.at[owner])
    for slot, source, k, first, other, height in col_plan:
        ref = pieces[slot]
        owner = lax.rem(y + k, y_count) * 2 + (1 - c if other else c)
        body = min(height, PAIR - first)
        at = pl.multiple_of(owner * PAIR + first, BLOCK)
        from_rows = pl.ds(source, body)
        copy(ref.at[from_rows, pl.ds(0, features)], cols_v.at[pl.ds(at, body)])
        copy(ref.at[from_rows, pl.ds(features, comps)], start_v.at[pl.ds(at, body)])
        if first + height > PAIR:
            copy(ref.at[pl.ds(source + body, EXTRA), pl.ds(0, BLOCK)], col_links.at[owner])
    for made in copies:
        made.wait()
    v_copy = pltpu.make_async_copy(start_v, v_out, out_sems.at[col_owners])
    v_copy.start()

    width = col_owners * PAIR
    lane = lax.broadcasted_iota(jnp.int32, (BLOCK, width), 1)
    place = lax.broadcasted_iota(jnp.int32, (BLOCK, width), 0)
    lane_owner = lane // PAIR
    lane_slab = ((lane_owner // 2) * z_count + z) * 2 + lane_owner % 2
    select = (place == lane_slab).astype(jnp.bfloat16)
    ahead_rows = jnp.concatenate([row_links[k][0:1] for k in range(row_owners)], axis=0)
    ahead = jnp.dot(ahead_rows, select, preferred_element_type=jnp.float32)
    spread_to = (place[:col_owners] == lane_owner[:col_owners]).astype(jnp.bfloat16)
    back_rows = jnp.concatenate([col_links[k][0:1] for k in range(col_owners)], axis=0)
    spread_back = lax.dot_general(
        back_rows, spread_to, (((0,), (0,)), ((), ())), preferred_element_type=jnp.float32
    ).astype(jnp.bfloat16)
    row_slab = (y * z_count + lax.broadcasted_iota(jnp.int32, (row_owners, BLOCK), 0)) * 2 + c
    row_pick = lax.broadcasted_iota(jnp.int32, (row_owners, BLOCK), 1) == row_slab
    back = jnp.dot(row_pick.astype(jnp.bfloat16), spread_back, preferred_element_type=jnp.float32)
    col_block = (xb + 2 * ((lane[:row_owners] // BLOCK) % 2)).astype(jnp.float32)
    same = (lane_owner[:row_owners] == y * 2 + c) & (place[:row_owners] == z)
    base = (ahead == col_block).astype(jnp.float32) + same.astype(jnp.float32)
    for half in range(2):
        row_block = (2 * xa + half).astype(jnp.float32)
        weight[half] = base + (back == row_block).astype(jnp.float32)

    factor = 2.0 / math.sqrt(features) * math.log2(math.e)

    def scale_of(values):
        wide = values.astype(jnp.float32)
        mean = jnp.sum(wide * wide, axis=-1, keepdims=True) * (1.0 / features)
        return lax.rsqrt(mean + EPSILON)

    row_scales = [
        scale_of(rows_v[pl.ds(i * PAIR, PAIR)]) * factor for i in range(row_owners)
    ]
    eye = lax.broadcasted_iota(jnp.int32, (BLOCK, BLOCK), 0) == lax.broadcasted_iota(
        jnp.int32, (BLOCK, BLOCK), 1
    )

    def out_copy(j):
        where = pl.ds(pl.multiple_of(j * PAIR, PAIR), PAIR)
        return pltpu.make_async_copy(w_v.at[:, where], w_out.at[:, where], out_sems.at[j])

    own_col = y * 2 + c

    def column(j, carry):
        at = pl.multiple_of(j * PAIR, PAIR)
        part = cols_v[pl.ds(at, PAIR)]
        scale = jnp.transpose(jnp.broadcast_to(scale_of(part), (PAIR, BLOCK)))[0:1]
        sums = [jnp.zeros((1, BLOCK), jnp.float32) for _ in range(2)]
        for i in range(row_owners):
            products = lax.dot_general(
                rows_v[i * PAIR : (i + 1) * PAIR],
                part,
                (((1,), (1,)), ((), ())),
                preferred_element_type=jnp.float32,
            )
            values = jnp.exp2(products * row_scales[i] * scale)
            for half in range(2):
                counts = weight[half, pl.ds(i, 1), pl.ds(at, PAIR)]
                for side in range(2):
                    block = values[half * BLOCK : (half + 1) * BLOCK, side * BLOCK : (side + 1) * BLOCK]
                    block = block * counts[:, side * BLOCK : (side + 1) * BLOCK]
                    block = block.astype(jnp.bfloat16)
                    w_v[
                        pl.ds(i * PAIR + half * BLOCK, BLOCK),
                        pl.ds(pl.multiple_of(at + side * BLOCK, BLOCK), BLOCK),
                    ] = block
                    sums[side] += jnp.sum(block.astype(jnp.float32), axis=0, keepdims=True)
        sums_out[:, pl.ds(at, PAIR)] = jnp.concatenate(sums, axis=1)

        @pl.when(j == own_col)
        def _():
            lanes = pl.ds(pl.multiple_of(at + xa * BLOCK, BLOCK), BLOCK)
            own_rows = pl.ds(pl.multiple_of(z * PAIR + xb * BLOCK, BLOCK), BLOCK)
            block = w_v[own_rows, lanes]
            w_v[own_rows, lanes] = jnp.where(eye, jnp.zeros_like(block), block)
            whole = w_v[:, lanes].astype(jnp.float32)
            sums_out[:, lanes] = jnp.sum(whole, axis=0, keepdims=True)

        out_copy(j).start()
        return carry

    lax.fori_loop(0, col_owners, column, 0)

    def drain(j, carry):
        out_copy(j).wait()
        return carry

    lax.fori_loop(0, col_owners, drain, 0)
    v_copy.wait()


def build_tile(row_pieces, col_pieces, ids, features, comps):
    y_count, z_count = lax.axis_size("y"), lax.axis_size("z")
    operands = []

    def slot_of(array):
        for slot, seen in enumerate(operands):
            if seen is array:
                return slot
        operands.append(array)
        return len(operands) - 1

    row_plan = [(slot_of(array), *rest) for array, *rest in row_pieces]
    col_plan = [(slot_of(array), *rest) for array, *rest in col_pieces]
    height, width = z_count * PAIR, 2 * y_count * PAIR
    copies = 2 * len(row_plan) + 3 * len(col_plan)
    kernel = functools.partial(
        tile_kernel, (len(operands), row_plan, col_plan), (y_count, z_count, features, comps)
    )
    return pl.pallas_call(
        kernel,
        out_shape=(
            jax.ShapeDtypeStruct((height, width), jnp.bfloat16),
            jax.ShapeDtypeStruct((1, width), jnp.float32),
            jax.ShapeDtypeStruct((width, comps), jnp.bfloat16),
        ),
        in_specs=[pl.BlockSpec(memory_space=pltpu.SMEM)]
        + [pl.BlockSpec(memory_space=pl.ANY)] * len(operands),
        out_specs=(
            pl.BlockSpec(memory_space=pl.ANY),
            pl.BlockSpec(memory_space=pltpu.VMEM),
            pl.BlockSpec(memory_space=pl.ANY),
        ),
        scratch_shapes=[
            pltpu.VMEM((height, features), jnp.bfloat16),
            pltpu.VMEM((width, features), jnp.bfloat16),
            pltpu.VMEM((width, comps), jnp.bfloat16),
            pltpu.VMEM((z_count, EXTRA, BLOCK), jnp.bfloat16),
            pltpu.VMEM((2 * y_count, EXTRA, BLOCK), jnp.bfloat16),
            pltpu.VMEM((2, z_count, width), jnp.float32),
            pltpu.VMEM((height, width), jnp.bfloat16),
            pltpu.SemaphoreType.DMA((copies,)),
            pltpu.SemaphoreType.DMA((2 * y_count + 1,)),
        ],
        compiler_params=pltpu.CompilerParams(vmem_limit_bytes=58 * 1024 * 1024),
        cost_estimate=pl.CostEstimate(
            flops=2 * height * width * features,
            bytes_accessed=2 * (height + width) * features + 2 * height * width,
            transcendentals=height * width,
        ),
        name="affinity_tile",
    )(ids, *operands)


def on_device(embed, start, links):
    slab_rows, features = embed.shape
    comps = start.shape[1]
    y_count, z_count = lax.axis_size("y"), lax.axis_size("z")
    y, z, c, xa, xb = (lax.axis_index(name) for name in ("y", "z", "c", "xa", "xb"))
    points = slab_rows * 2 * y_count * z_count
    highest = lax.Precision.HIGHEST

    note = jnp.pad(links.astype(jnp.bfloat16), ((0, EXTRA - 1), (0, BLOCK - links.shape[1])))
    row_own = lax.dynamic_slice_in_dim(embed, xa * PAIR, PAIR, 0)
    row_own = jnp.concatenate(
        [row_own, jnp.pad(note, ((0, 0), (0, features - BLOCK)))], axis=0
    )

    def blocks_of(values):
        shaped = values.reshape(2, 2, BLOCK, values.shape[1])
        return lax.dynamic_index_in_dim(shaped, xb, 1, keepdims=False).reshape(PAIR, -1)

    col_own = jnp.concatenate([blocks_of(embed), blocks_of(start)], axis=1)
    col_own = jnp.concatenate(
        [col_own, jnp.pad(note, ((0, 0), (0, features + comps - BLOCK)))], axis=0
    )
    row_pieces, col_pieces = exchange(row_own, col_own)
    ids = jnp.stack([y, z, c, xa, xb]).astype(jnp.int32)
    tile, sums, fetched_start = build_tile(row_pieces, col_pieces, ids, features, comps)

    sums = sums + lax.ppermute(sums, "xa", [(0, 1), (1, 0)])
    inv_root_cols = lax.rsqrt(total_of(sums, ("y", "c")))[0]
    own_at = (y * 2 + c) * PAIR + xa * BLOCK
    inv_root = lax.dynamic_slice_in_dim(inv_root_cols, own_at, BLOCK, 0)[:, None]
    fetched = (fetched_start.astype(jnp.float32) * inv_root_cols[:, None]).astype(jnp.bfloat16)
    for turn in range(ITERS):
        part = jnp.dot(tile, fetched, preferred_element_type=jnp.float32).astype(jnp.bfloat16)
        parts = part.reshape(-1, BLOCK, comps)
        got = lax.all_to_all(parts, ROW_GROUP, split_axis=0, concat_axis=0, tiled=True)
        result = jnp.sum(got.astype(jnp.float32), axis=0) * inv_root
        gram = gram_total(jnp.dot(result.T, result, precision=highest))
        if turn == ITERS - 1:
            result = from_everyone(result, ("xa", "xb")).reshape(slab_rows, comps)
            return orthonormal(result, gram) * math.sqrt(points)
        current = orthonormal(result, gram)
        scaled = (current * inv_root).astype(jnp.bfloat16)
        fetched = from_everyone(scaled, COL_GROUP).reshape(-1, comps)


def solution(mesh):
    owners, reps = mesh.devices.shape
    side = math.isqrt(owners // 2)
    fine = Mesh(mesh.devices.reshape(side, side, 2, 2, reps // 2), ("y", "z", "c", "xa", "xb"))
    return jax.shard_map(
        on_device,
        mesh=fine,
        in_specs=(P(ROWS, None), P(ROWS, None), P(ROWS, None)),
        out_specs=P(ROWS, None),
        check_vma=False,
    )
```

profile of v0, /device:TPU:1, one launch (start us, length us, event | category | flops | bytes accessed | tf_op | source)
XLA Modules:
  0.0 393.8 jit_solution(7000458318026190889)
XLA Ops:
  0.0 0.7 convert_element_type.30
  0.8 0.8 constant_dynamic-slice_fusion
  1.7 5.9 %collective-permute-start.11 = (bf16[264,1152]{1,0:T(8,128)(2,1)S(1)}, bf16[264,1152]{1,0:T(8,128)(2,1)S(1)}, u32[]{:S(2)}, u32[]{:S(2)}) collective-permute-start(bf16[264,1152]{1,0:T(8,128)(2,1)S(1)} %fusion.4.refs_9_), channel_id=1, source_target_pairs={{0,448},{64,0},{128,64},{192,128},{256,192},{320,256},{384,320},{4... | collective-permute-start | bytes 1824776 | tf_op jit(solution)/shard_map/ppermute | solution.py:123
  7.7 10.7 %collective-permute-start.1 = (bf16[264,1024]{1,0:T(8,128)(2,1)S(1)}, bf16[264,1024]{1,0:T(8,128)(2,1)S(1)}, u32[]{:S(2)}, u32[]{:S(2)}) collective-permute-start(bf16[264,1024]{1,0:T(8,128)(2,1)S(1)} %fusion.5.refs_0_), channel_id=1, source_target_pairs={{0,56},{8,0},{16,8},{24,16},{32,24},{40,32},{48,40},{56,48},{1,57}... | collective-permute-start | bytes 1622024 | tf_op jit(solution)/shard_map/ppermute | solution.py:125
  18.4 1.9 collective-permute-start.9
  20.4 3.1 collective-permute-start.8
  23.5 4.9 %collective-permute-start.15 = (bf16[264,1152]{1,0:T(8,128)(2,1)S(1)}, bf16[264,1152]{1,0:T(8,128)(2,1)S(1)}, u32[]{:S(2)}, u32[]{:S(2)}) collective-permute-start(bf16[264,1152]{1,0:T(8,128)(2,1)S(1)} %collective-permute-done.11.refs_13_), channel_id=1, source_target_pairs={{0,448},{64,0},{128,64},{192,128},{256,192},{320,256},{384,320},{4... | collective-permute-start | bytes 1824776 | tf_op jit(solution)/shard_map/ppermute | solution.py:123
  28.4 1.9 collective-permute-start
  30.3 7.6 %collective-permute-start.3 = (bf16[264,1024]{1,0:T(8,128)(2,1)S(1)}, bf16[264,1024]{1,0:T(8,128)(2,1)S(1)}, u32[]{:S(2)}, u32[]{:S(2)}) collective-permute-start(bf16[264,1024]{1,0:T(8,128)(2,1)S(1)} %collective-permute-done.1.refs_2_), channel_id=1, source_target_pairs={{0,56},{8,0},{16,8},{24,16},{32,24},{40,32},{48,40},{56,48},{1,57}... | collective-permute-start | bytes 1622024 | tf_op jit(solution)/shard_map/ppermute | solution.py:125
  38.0 1.9 collective-permute-start.13
  39.9 6.9 %collective-permute-done.refs_1_ = bf16[264,1024]{1,0:T(8,128)(2,1)S(1)} collective-permute-done((bf16[264,1024]{1,0:T(8,128)(2,1)S(1)}, bf16[264,1024]{1,0:T(8,128)(2,1)S(1)}, u32[]{:S(2)}, u32[]{:S(2)}) %collective-permute-start) | collective-permute-done | bytes 540704 | tf_op jit(solution)/shard_map/ppermute | solution.py:124
  46.8 4.3 %collective-permute-start.12 = (bf16[264,1152]{1,0:T(8,128)(2,1)S(1)}, bf16[264,1152]{1,0:T(8,128)(2,1)S(1)}, u32[]{:S(2)}, u32[]{:S(2)}) collective-permute-start(bf16[264,1152]{1,0:T(8,128)(2,1)S(1)} %collective-permute-done.11.refs_13_), channel_id=1, source_target_pairs={{0,4},{4,0},{1,5},{5,1},{2,6},{6,2},{3,7},{7,3},{8,12},{12,8},{9,1... | collective-permute-start | bytes 1824776 | tf_op jit(solution)/shard_map/ppermute | solution.py:114
  51.2 1.9 collective-permute-start.10
  53.1 1.9 collective-permute-start.19
  55.1 1.9 collective-permute-start.2
  57.0 3.4 collective-permute-start.17
  60.4 10.9 %collective-permute-done.2.refs_3_ = bf16[264,1024]{1,0:T(8,128)(2,1)S(1)} collective-permute-done((bf16[264,1024]{1,0:T(8,128)(2,1)S(1)}, bf16[264,1024]{1,0:T(8,128)(2,1)S(1)}, u32[]{:S(2)}, u32[]{:S(2)}) %collective-permute-start.2) | collective-permute-done | bytes 540704 | tf_op jit(solution)/shard_map/ppermute | solution.py:124
  71.3 3.4 collective-permute-start.16
  74.8 2.2 collective-permute-start.5
  77.0 2.2 collective-permute-start.14
  79.3 3.1 collective-permute-start.4
  82.4 8.1 %collective-permute-done.5.refs_6_ = bf16[264,1024]{1,0:T(8,128)(2,1)S(1)} collective-permute-done((bf16[264,1024]{1,0:T(8,128)(2,1)S(1)}, bf16[264,1024]{1,0:T(8,128)(2,1)S(1)}, u32[]{:S(2)}, u32[]{:S(2)}) %collective-permute-start.5) | collective-permute-done | bytes 540704 | tf_op jit(solution)/shard_map/ppermute | solution.py:125
  90.5 2.8 collective-permute-start.23
  93.3 2.6 collective-permute-done.4.refs_5_
  96.0 3.0 collective-permute-start.20
  99.0 1.9 collective-permute-start.18
  100.9 1.0 slice.18
  101.9 3.4 collective-permute-start.21
  105.3 1.9 collective-permute-start.6
  107.3 3.0 collective-permute-start.24
  110.3 2.9 collective-permute-done.21.refs_23_
  113.2 3.3 collective-permute-start.22
  116.6 0.7 copy-done.20
  117.3 1.9 collective-permute-start.7
  119.2 0.6 stack.23.ids
  119.8 7.0 %collective-permute-done.7.refs_8_ = bf16[136,1024]{1,0:T(8,128)(2,1)} collective-permute-done((bf16[136,1024]{1,0:T(8,128)(2,1)S(1)}, bf16[136,1024]{1,0:T(8,128)(2,1)}, u32[]{:S(2)}, u32[]{:S(2)}) %collective-permute-start.7) | collective-permute-done | bytes 278560 | tf_op jit(solution)/shard_map/ppermute | solution.py:134
  126.9 38.8 %affinity_tile.1 = (bf16[2048,4096]{1,0:T(8,128)(2,1)}, f32[1,4096]{1,0:T(1,128)}, bf16[4096,128]{1,0:T(8,128)(2,1)}) custom-call(s32[5]{0:T(128)} %stack.23.ids, bf16[264,1024]{1,0:T(8,128)(2,1)} %copy-done.2, bf16[264,1024]{1,0:T(8,128)(2,1)} %copy-done.16, bf16[264,1024]{1,0:T(8,128)(2,1)} %copy-done.15, bf16[264,1024]{1,0:T(8,128)(2,1)} %copy-done.18, ...), custom_call_target="tpu_custom_call" | custom-call | flops 17179869184 | bytes 29360128 | tf_op jit(solution)/shard_map/affinity_tile/pallas_call | solution.py:288
  165.7 4.6 %collective-permute-start.25 = (f32[1,4096]{1,0:T(1,128)}, f32[1,4096]{1,0:T(1,128)S(1)}, u32[]{:S(2)}, u32[]{:S(2)}) collective-permute-start(f32[1,4096]{1,0:T(1,128)} %get-tuple-element.10), channel_id=1, source_target_pairs={{0,2},{2,0},{1,3},{3,1},{4,6},{6,4},{5,7},{7,5},{8,10},{10,8},{9,1... | collective-permute-start | bytes 49160 | tf_op jit(solution)/shard_map/ppermute | solution.py:349
  170.3 1.6 collective-permute-done.25
  171.9 0.7 add.31
  172.6 0.2 broadcast_in_dim.22
  172.8 18.1 %all_to_all.55 = f32[16,1,4096]{2,1,0:T(1,128)S(1)} all-to-all(f32[16,1,4096]{2,1,0:T(1,128)S(1)} %broadcast_in_dim.22), channel_id=1, replica_groups=mesh['y'=8,'z'=8,'c'=2,'xa'=2,'xb'=2] {'y','c'}, dimensions={0} | all-to-all | bytes 524288 | tf_op jit(solution)/shard_map/all_to_all | solution.py:25
  191.0 0.2 reduce_sum.63
  191.2 11.5 %convolution_convert_fusion.1 = bf16[2048,128]{1,0:T(8,128)(2,1)} fusion(bf16[2048,4096]{1,0:T(8,128)(2,1)} %get-tuple-element.8, bf16[4096,128]{1,0:T(8,128)(2,1)} %get-tuple-element.9, f32[4096]{0:T(1024)S(1)} %rsqrt.16), kind=kOutput, calls=%fused_computation.1 | convolution fusion | flops 2149318656 | bytes 18366464 | tf_op jit(solution)/shard_map/dot_general | solution.py:355
  202.6 4.4 %all-to-all-start.1 = ((bf16[16,128,128]{2,1,0:T(8,128)(2,1)}), bf16[16,128,128]{2,1,0:T(8,128)(2,1)S(1)}, u32[]{:S(2)}, u32[]{:S(2)}) async-start(bf16[16,128,128]{2,1,0:T(8,128)(2,1)} %bitcast.10), calls=%async_computation.1 | async-start | bytes 1048576 | tf_op jit(solution)/shard_map/all_to_all | solution.py:357
  207.2 16.4 %all-to-all-done.1 = bf16[16,128,128]{2,1,0:T(8,128)(2,1)S(1)} async-done(((bf16[16,128,128]{2,1,0:T(8,128)(2,1)}), bf16[16,128,128]{2,1,0:T(8,128)(2,1)S(1)}, u32[]{:S(2)}, u32[]{:S(2)}) %all-to-all-start.1) | async-done | bytes 524320 | tf_op jit(solution)/shard_map/all_to_all | solution.py:357
  223.6 0.4 fusion.7
  224.0 15.1 %all_to_all.56 = f32[32,4,128]{2,1,0:T(4,128)S(1)} all-to-all(f32[32,4,128]{2,1,0:T(4,128)S(1)} %bitcast.39), channel_id=1, replica_groups=mesh['y'=8,'z'=8,'c'=2,'xa'=2,'xb'=2] {'z','xa','xb'}, dimensions={0} | all-to-all | bytes 131072 | tf_op jit(solution)/shard_map/all_to_all | solution.py:35
  239.2 11.8 %all_to_all.57 = f32[16,4,128]{2,1,0:T(4,128)S(1)} all-to-all(f32[16,4,128]{2,1,0:T(4,128)S(1)} %broadcast_in_dim.23), channel_id=1, replica_groups=mesh['y'=8,'z'=8,'c'=2,'xa'=2,'xb'=2] {'y','c'}, dimensions={0} | all-to-all | bytes 65536 | tf_op jit(solution)/shard_map/all_to_all | solution.py:25
  251.0 12.5 %all_to_all.58 = f32[32,4,128]{2,1,0:T(4,128)} all-to-all(f32[32,4,128]{2,1,0:T(4,128)S(1)} %broadcast_in_dim.24), channel_id=1, replica_groups=mesh['y'=8,'z'=8,'c'=2,'xa'=2,'xb'=2] {'z','xa','xb'}, dimensions={0} | all-to-all | bytes 131072 | tf_op jit(solution)/shard_map/all_to_all | solution.py:25
  263.5 11.1 %inverse_factor.2 = f32[128,128]{1,0:T(8,128)} custom-call(f32[128,128]{1,0:T(8,128)} %bitcast.38), custom_call_target="tpu_custom_call" | custom-call | tf_op jit(solution)/shard_map/inverse_factor/pallas_call | solution.py:88
  274.6 1.1 fusion.1
  275.8 0.2 broadcast_in_dim.25
  276.0 32.7 %all_to_all.59 = bf16[32,128,128]{2,1,0:T(8,128)(2,1)S(1)} all-to-all(bf16[32,128,128]{2,1,0:T(8,128)(2,1)S(1)} %broadcast_in_dim.25), channel_id=1, replica_groups=mesh['y'=8,'z'=8,'c'=2,'xa'=2,'xb'=2] {'y','c','xa'}, dimensions={0} | all-to-all | bytes 2097152 | tf_op jit(solution)/shard_map/all_to_all | solution.py:25
  308.7 8.2 %convolution_convert_fusion = bf16[2048,128]{1,0:T(8,128)(2,1)S(1)} fusion(bf16[2048,4096]{1,0:T(8,128)(2,1)} %get-tuple-element.8, bf16[4096,128]{1,0:T(8,128)(2,1)S(1)} %bitcast.32), kind=kOutput, calls=%fused_computation | convolution fusion | flops 2147745792 | bytes 18350080 | tf_op jit(solution)/shard_map/dot_general | solution.py:355
  316.9 18.3 %all_to_all.60 = bf16[16,128,128]{2,1,0:T(8,128)(2,1)S(1)} all-to-all(bf16[16,128,128]{2,1,0:T(8,128)(2,1)S(1)} %bitcast.34), channel_id=1, replica_groups=mesh['y'=8,'z'=8,'c'=2,'xa'=2,'xb'=2] {'z','xb'}, dimensions={0} | all-to-all | bytes 1048576 | tf_op jit(solution)/shard_map/all_to_all | solution.py:357
  335.3 0.3 fusion.11
  335.6 16.6 %all_to_all.61 = f32[32,4,128]{2,1,0:T(4,128)S(1)} all-to-all(f32[32,4,128]{2,1,0:T(4,128)S(1)} %bitcast.36), channel_id=1, replica_groups=mesh['y'=8,'z'=8,'c'=2,'xa'=2,'xb'=2] {'z','xa','xb'}, dimensions={0} | all-to-all | bytes 131072 | tf_op jit(solution)/shard_map/all_to_all | solution.py:35
  352.3 11.8 %all_to_all.62 = f32[16,4,128]{2,1,0:T(4,128)S(1)} all-to-all(f32[16,4,128]{2,1,0:T(4,128)S(1)} %broadcast_in_dim.27), channel_id=1, replica_groups=mesh['y'=8,'z'=8,'c'=2,'xa'=2,'xb'=2] {'y','c'}, dimensions={0} | all-to-all | bytes 65536 | tf_op jit(solution)/shard_map/all_to_all | solution.py:25
  364.2 12.5 %all_to_all.63 = f32[32,4,128]{2,1,0:T(4,128)} all-to-all(f32[32,4,128]{2,1,0:T(4,128)S(1)} %broadcast_in_dim.28), channel_id=1, replica_groups=mesh['y'=8,'z'=8,'c'=2,'xa'=2,'xb'=2] {'z','xa','xb'}, dimensions={0} | all-to-all | bytes 131072 | tf_op jit(solution)/shard_map/all_to_all | solution.py:25
  376.7 0.7 broadcast_in_dim.26
  377.4 3.4 all-to-all-start.7
  380.8 11.1 %inverse_factor.3 = f32[128,128]{1,0:T(8,128)} custom-call(f32[128,128]{1,0:T(8,128)} %bitcast.37), custom_call_target="tpu_custom_call" | custom-call | tf_op jit(solution)/shard_map/inverse_factor/pallas_call | solution.py:88
  391.9 1.9 convolution_multiply_fusion
  (82 shorter events, 0.9 us)
Async XLA Ops:
  0.0 1.6 copy-start
  1.7 80.7 %copy-start.1 = (bf16[264,1152]{1,0:T(8,128)(2,1)}, bf16[264,1152]{1,0:T(8,128)(2,1)S(1)}, u32[]{:S(2)}) copy-start(bf16[264,1152]{1,0:T(8,128)(2,1)S(1)} %fusion.4.refs_9_) | copy-start | bytes 1824772
  1.7 21.8 %collective-permute-start.11 = (bf16[264,1152]{1,0:T(8,128)(2,1)S(1)}, bf16[264,1152]{1,0:T(8,128)(2,1)S(1)}, u32[]{:S(2)}, u32[]{:S(2)}) collective-permute-start(bf16[264,1152]{1,0:T(8,128)(2,1)S(1)} %fusion.4.refs_9_), channel_id=1, source_target_pairs={{0,448},{64,0},{128,64},{192,128},{256,192},{320,256},{384,320},{4... | collective-permute-start | bytes 1824776 | tf_op jit(solution)/shard_map/ppermute | solution.py:123
  7.7 119.1 %copy-start.2 = (bf16[264,1024]{1,0:T(8,128)(2,1)}, bf16[264,1024]{1,0:T(8,128)(2,1)S(1)}, u32[]{:S(2)}) copy-start(bf16[264,1024]{1,0:T(8,128)(2,1)S(1)} %fusion.5.refs_0_) | copy-start | bytes 1622020
  7.7 22.6 %collective-permute-start.1 = (bf16[264,1024]{1,0:T(8,128)(2,1)S(1)}, bf16[264,1024]{1,0:T(8,128)(2,1)S(1)}, u32[]{:S(2)}, u32[]{:S(2)}) collective-permute-start(bf16[264,1024]{1,0:T(8,128)(2,1)S(1)} %fusion.5.refs_0_), channel_id=1, source_target_pairs={{0,56},{8,0},{16,8},{24,16},{32,24},{40,32},{48,40},{56,48},{1,57}... | collective-permute-start | bytes 1622024 | tf_op jit(solution)/shard_map/ppermute | solution.py:125
  18.4 19.5 %collective-permute-start.9 = (bf16[264,1152]{1,0:T(8,128)(2,1)S(1)}, bf16[264,1152]{1,0:T(8,128)(2,1)S(1)}, u32[]{:S(2)}, u32[]{:S(2)}) collective-permute-start(bf16[264,1152]{1,0:T(8,128)(2,1)S(1)} %fusion.4.refs_9_), channel_id=1, source_target_pairs={{0,64},{64,128},{128,192},{192,256},{256,320},{320,384},{384,448},... | collective-permute-start | bytes 1824776 | tf_op jit(solution)/shard_map/ppermute | solution.py:122
  20.4 30.8 %collective-permute-start.8 = (bf16[264,1152]{1,0:T(8,128)(2,1)S(1)}, bf16[264,1152]{1,0:T(8,128)(2,1)S(1)}, u32[]{:S(2)}, u32[]{:S(2)}) collective-permute-start(bf16[264,1152]{1,0:T(8,128)(2,1)S(1)} %fusion.4.refs_9_), channel_id=1, source_target_pairs={{0,4},{4,0},{1,5},{5,1},{2,6},{6,2},{3,7},{7,3},{8,12},{12,8},{9,1... | collective-permute-start | bytes 1824776 | tf_op jit(solution)/shard_map/ppermute | solution.py:114
  23.5 51.3 %copy-start.6 = (bf16[264,1152]{1,0:T(8,128)(2,1)}, bf16[264,1152]{1,0:T(8,128)(2,1)S(1)}, u32[]{:S(2)}) copy-start(bf16[264,1152]{1,0:T(8,128)(2,1)S(1)} %collective-permute-done.11.refs_13_) | copy-start | bytes 1824772
  23.5 29.6 %collective-permute-start.15 = (bf16[264,1152]{1,0:T(8,128)(2,1)S(1)}, bf16[264,1152]{1,0:T(8,128)(2,1)S(1)}, u32[]{:S(2)}, u32[]{:S(2)}) collective-permute-start(bf16[264,1152]{1,0:T(8,128)(2,1)S(1)} %collective-permute-done.11.refs_13_), channel_id=1, source_target_pairs={{0,448},{64,0},{128,64},{192,128},{256,192},{320,256},{384,320},{4... | collective-permute-start | bytes 1824776 | tf_op jit(solution)/shard_map/ppermute | solution.py:123
  28.4 18.5 %collective-permute-start = (bf16[264,1024]{1,0:T(8,128)(2,1)S(1)}, bf16[264,1024]{1,0:T(8,128)(2,1)S(1)}, u32[]{:S(2)}, u32[]{:S(2)}) collective-permute-start(bf16[264,1024]{1,0:T(8,128)(2,1)S(1)} %fusion.5.refs_0_), channel_id=1, source_target_pairs={{0,8},{8,16},{16,24},{24,32},{32,40},{40,48},{48,56},{56,0},{1,9},... | collective-permute-start | bytes 1622024 | tf_op jit(solution)/shard_map/ppermute | solution.py:124
  30.3 48.9 %copy-start.15 = (bf16[264,1024]{1,0:T(8,128)(2,1)}, bf16[264,1024]{1,0:T(8,128)(2,1)S(1)}, u32[]{:S(2)}) copy-start(bf16[264,1024]{1,0:T(8,128)(2,1)S(1)} %collective-permute-done.1.refs_2_) | copy-start | bytes 1622020
  30.3 24.7 %collective-permute-start.3 = (bf16[264,1024]{1,0:T(8,128)(2,1)S(1)}, bf16[264,1024]{1,0:T(8,128)(2,1)S(1)}, u32[]{:S(2)}, u32[]{:S(2)}) collective-permute-start(bf16[264,1024]{1,0:T(8,128)(2,1)S(1)} %collective-permute-done.1.refs_2_), channel_id=1, source_target_pairs={{0,56},{8,0},{16,8},{24,16},{32,24},{40,32},{48,40},{56,48},{1,57}... | collective-permute-start | bytes 1622024 | tf_op jit(solution)/shard_map/ppermute | solution.py:125
  38.0 41.2 %copy-start.7 = (bf16[264,1152]{1,0:T(8,128)(2,1)}, bf16[264,1152]{1,0:T(8,128)(2,1)S(1)}, u32[]{:S(2)}) copy-start(bf16[264,1152]{1,0:T(8,128)(2,1)S(1)} %collective-permute-done.9.refs_11_) | copy-start | bytes 1824772
  38.0 19.0 %collective-permute-start.13 = (bf16[264,1152]{1,0:T(8,128)(2,1)S(1)}, bf16[264,1152]{1,0:T(8,128)(2,1)S(1)}, u32[]{:S(2)}, u32[]{:S(2)}) collective-permute-start(bf16[264,1152]{1,0:T(8,128)(2,1)S(1)} %collective-permute-done.9.refs_11_), channel_id=1, source_target_pairs={{0,64},{64,128},{128,192},{192,256},{256,320},{320,384},{384,448},... | collective-permute-start | bytes 1824776 | tf_op jit(solution)/shard_map/ppermute | solution.py:122
  46.8 32.4 %copy-start.16 = (bf16[264,1024]{1,0:T(8,128)(2,1)}, bf16[264,1024]{1,0:T(8,128)(2,1)S(1)}, u32[]{:S(2)}) copy-start(bf16[264,1024]{1,0:T(8,128)(2,1)S(1)} %collective-permute-done.refs_1_) | copy-start | bytes 1622020
  46.8 27.9 %collective-permute-start.12 = (bf16[264,1152]{1,0:T(8,128)(2,1)S(1)}, bf16[264,1152]{1,0:T(8,128)(2,1)S(1)}, u32[]{:S(2)}, u32[]{:S(2)}) collective-permute-start(bf16[264,1152]{1,0:T(8,128)(2,1)S(1)} %collective-permute-done.11.refs_13_), channel_id=1, source_target_pairs={{0,4},{4,0},{1,5},{5,1},{2,6},{6,2},{3,7},{7,3},{8,12},{12,8},{9,1... | collective-permute-start | bytes 1824776 | tf_op jit(solution)/shard_map/ppermute | solution.py:114
  51.1 1.9 copy-start.8
  51.2 25.8 %collective-permute-start.10 = (bf16[264,1152]{1,0:T(8,128)(2,1)S(1)}, bf16[264,1152]{1,0:T(8,128)(2,1)S(1)}, u32[]{:S(2)}, u32[]{:S(2)}) collective-permute-start(bf16[264,1152]{1,0:T(8,128)(2,1)S(1)} %collective-permute-done.9.refs_11_), channel_id=1, source_target_pairs={{0,4},{4,0},{1,5},{5,1},{2,6},{6,2},{3,7},{7,3},{8,12},{12,8},{9,1... | collective-permute-start | bytes 1824776 | tf_op jit(solution)/shard_map/ppermute | solution.py:114
  53.1 63.4 %copy-start.9 = (bf16[264,1152]{1,0:T(8,128)(2,1)}, bf16[264,1152]{1,0:T(8,128)(2,1)S(1)}, u32[]{:S(2)}) copy-start(bf16[264,1152]{1,0:T(8,128)(2,1)S(1)} %collective-permute-done.15.refs_17_) | copy-start | bytes 1824772
  53.1 26.1 %collective-permute-start.19 = (bf16[264,1152]{1,0:T(8,128)(2,1)S(1)}, bf16[264,1152]{1,0:T(8,128)(2,1)S(1)}, u32[]{:S(2)}, u32[]{:S(2)}) collective-permute-start(bf16[264,1152]{1,0:T(8,128)(2,1)S(1)} %collective-permute-done.15.refs_17_), channel_id=1, source_target_pairs={{0,448},{64,0},{128,64},{192,128},{256,192},{320,256},{384,320},{4... | collective-permute-start | bytes 1824776 | tf_op jit(solution)/shard_map/ppermute | solution.py:123
  55.1 43.9 %copy-start.17 = (bf16[264,1024]{1,0:T(8,128)(2,1)}, bf16[264,1024]{1,0:T(8,128)(2,1)S(1)}, u32[]{:S(2)}) copy-start(bf16[264,1024]{1,0:T(8,128)(2,1)S(1)} %collective-permute-done.3.refs_4_) | copy-start | bytes 1622020
  55.1 16.3 %collective-permute-start.2 = (bf16[264,1024]{1,0:T(8,128)(2,1)S(1)}, bf16[264,1024]{1,0:T(8,128)(2,1)S(1)}, u32[]{:S(2)}, u32[]{:S(2)}) collective-permute-start(bf16[264,1024]{1,0:T(8,128)(2,1)S(1)} %collective-permute-done.refs_1_), channel_id=1, source_target_pairs={{0,8},{8,16},{16,24},{24,32},{32,40},{40,48},{48,56},{56,0},{1,9},... | collective-permute-start | bytes 1622024 | tf_op jit(solution)/shard_map/ppermute | solution.py:124
  57.0 59.5 %copy-start.10 = (bf16[264,1152]{1,0:T(8,128)(2,1)}, bf16[264,1152]{1,0:T(8,128)(2,1)S(1)}, u32[]{:S(2)}) copy-start(bf16[264,1152]{1,0:T(8,128)(2,1)S(1)} %collective-permute-done.13.refs_15_) | copy-start | bytes 1824772
  57.0 41.9 %collective-permute-start.17 = (bf16[264,1152]{1,0:T(8,128)(2,1)S(1)}, bf16[264,1152]{1,0:T(8,128)(2,1)}, u32[]{:S(2)}, u32[]{:S(2)}) collective-permute-start(bf16[264,1152]{1,0:T(8,128)(2,1)S(1)} %collective-permute-done.13.refs_15_), channel_id=1, source_target_pairs={{0,64},{64,128},{128,192},{192,256},{256,320},{320,384},{384,448},... | collective-permute-start | bytes 1824776 | tf_op jit(solution)/shard_map/ppermute | solution.py:122
  71.3 45.2 %copy-start.18 = (bf16[264,1024]{1,0:T(8,128)(2,1)}, bf16[264,1024]{1,0:T(8,128)(2,1)S(1)}, u32[]{:S(2)}) copy-start(bf16[264,1024]{1,0:T(8,128)(2,1)S(1)} %collective-permute-done.2.refs_3_) | copy-start | bytes 1622020
  71.3 30.6 %collective-permute-start.16 = (bf16[264,1152]{1,0:T(8,128)(2,1)S(1)}, bf16[264,1152]{1,0:T(8,128)(2,1)S(1)}, u32[]{:S(2)}, u32[]{:S(2)}) collective-permute-start(bf16[264,1152]{1,0:T(8,128)(2,1)S(1)} %collective-permute-done.15.refs_17_), channel_id=1, source_target_pairs={{0,4},{4,0},{1,5},{5,1},{2,6},{6,2},{3,7},{7,3},{8,12},{12,8},{9,1... | collective-permute-start | bytes 1824776 | tf_op jit(solution)/shard_map/ppermute | solution.py:114
  74.8 4.4 %copy-start.11 = (bf16[264,1152]{1,0:T(8,128)(2,1)}, bf16[264,1152]{1,0:T(8,128)(2,1)S(1)}, u32[]{:S(2)}) copy-start(bf16[264,1152]{1,0:T(8,128)(2,1)S(1)} %collective-permute-done.12.refs_14_) | copy-start | bytes 1824772
  74.8 15.7 %collective-permute-start.5 = (bf16[264,1024]{1,0:T(8,128)(2,1)S(1)}, bf16[264,1024]{1,0:T(8,128)(2,1)S(1)}, u32[]{:S(2)}, u32[]{:S(2)}) collective-permute-start(bf16[264,1024]{1,0:T(8,128)(2,1)S(1)} %collective-permute-done.3.refs_4_), channel_id=1, source_target_pairs={{0,56},{8,0},{16,8},{24,16},{32,24},{40,32},{48,40},{56,48},{1,57}... | collective-permute-start | bytes 1622024 | tf_op jit(solution)/shard_map/ppermute | solution.py:125
  77.0 2.3 copy-start.12
  77.0 28.3 %collective-permute-start.14 = (bf16[264,1152]{1,0:T(8,128)(2,1)S(1)}, bf16[264,1152]{1,0:T(8,128)(2,1)S(1)}, u32[]{:S(2)}, u32[]{:S(2)}) collective-permute-start(bf16[264,1152]{1,0:T(8,128)(2,1)S(1)} %collective-permute-done.13.refs_15_), channel_id=1, source_target_pairs={{0,4},{4,0},{1,5},{5,1},{2,6},{6,2},{3,7},{7,3},{8,12},{12,8},{9,1... | collective-permute-start | bytes 1824776 | tf_op jit(solution)/shard_map/ppermute | solution.py:114
  79.2 47.6 %copy-start.3 = (bf16[264,1152]{1,0:T(8,128)(2,1)}, bf16[264,1152]{1,0:T(8,128)(2,1)S(1)}, u32[]{:S(2)}) copy-start(bf16[264,1152]{1,0:T(8,128)(2,1)S(1)} %collective-permute-done.19.refs_21_) | copy-start | bytes 1824772
  79.3 16.7 %collective-permute-start.4 = (bf16[264,1024]{1,0:T(8,128)(2,1)S(1)}, bf16[264,1024]{1,0:T(8,128)(2,1)S(1)}, u32[]{:S(2)}, u32[]{:S(2)}) collective-permute-start(bf16[264,1024]{1,0:T(8,128)(2,1)S(1)} %collective-permute-done.2.refs_3_), channel_id=1, source_target_pairs={{0,8},{8,16},{16,24},{24,32},{32,40},{40,48},{48,56},{56,0},{1,9},... | collective-permute-start | bytes 1622024 | tf_op jit(solution)/shard_map/ppermute | solution.py:124
  90.5 36.4 %copy-start.4 = (bf16[264,1024]{1,0:T(8,128)(2,1)}, bf16[264,1024]{1,0:T(8,128)(2,1)S(1)}, u32[]{:S(2)}) copy-start(bf16[264,1024]{1,0:T(8,128)(2,1)S(1)} %collective-permute-done.5.refs_6_) | copy-start | bytes 1622020
  90.5 16.8 %collective-permute-start.23 = (bf16[136,1152]{1,0:T(8,128)(2,1)S(1)}, bf16[136,1152]{1,0:T(8,128)(2,1)S(1)}, u32[]{:S(2)}, u32[]{:S(2)}) collective-permute-start(bf16[136,1152]{1,0:T(8,128)(2,1)S(1)} %slice.19), channel_id=1, source_target_pairs={{0,448},{64,0},{128,64},{192,128},{256,192},{320,256},{384,320},{4... | collective-permute-start | bytes 940040 | tf_op jit(solution)/shard_map/ppermute | solution.py:132
  96.0 20.6 %copy-start.5 = (bf16[264,1024]{1,0:T(8,128)(2,1)}, bf16[264,1024]{1,0:T(8,128)(2,1)S(1)}, u32[]{:S(2)}) copy-start(bf16[264,1024]{1,0:T(8,128)(2,1)S(1)} %collective-permute-done.4.refs_5_) | copy-start | bytes 1622020
  96.0 30.8 %collective-permute-start.20 = (bf16[264,1152]{1,0:T(8,128)(2,1)S(1)}, bf16[264,1152]{1,0:T(8,128)(2,1)}, u32[]{:S(2)}, u32[]{:S(2)}) collective-permute-start(bf16[264,1152]{1,0:T(8,128)(2,1)S(1)} %collective-permute-done.19.refs_21_), channel_id=1, source_target_pairs={{0,4},{4,0},{1,5},{5,1},{2,6},{6,2},{3,7},{7,3},{8,12},{12,8},{9,1... | collective-permute-start | bytes 1824776 | tf_op jit(solution)/shard_map/ppermute | solution.py:114
  99.0 27.9 %collective-permute-start.18 = (bf16[264,1152]{1,0:T(8,128)(2,1)}, bf16[264,1152]{1,0:T(8,128)(2,1)}, u32[]{:S(2)}, u32[]{:S(2)}) collective-permute-start(bf16[264,1152]{1,0:T(8,128)(2,1)} %collective-permute-done.17.refs_19_), channel_id=1, source_target_pairs={{0,4},{4,0},{1,5},{5,1},{2,6},{6,2},{3,7},{7,3},{8,12},{12,8},{9,1... | collective-permute-start | bytes 1824776 | tf_op jit(solution)/shard_map/ppermute | solution.py:114
  101.9 14.6 %copy-start.13 = (bf16[264,1152]{1,0:T(8,128)(2,1)}, bf16[264,1152]{1,0:T(8,128)(2,1)S(1)}, u32[]{:S(2)}) copy-start(bf16[264,1152]{1,0:T(8,128)(2,1)S(1)} %collective-permute-done.16.refs_18_) | copy-start | bytes 1824772
  101.9 11.3 %collective-permute-start.21 = (bf16[128,1152]{1,0:T(8,128)(2,1)S(1)}, bf16[128,1152]{1,0:T(8,128)(2,1)}, u32[]{:S(2)}, u32[]{:S(2)}) collective-permute-start(bf16[128,1152]{1,0:T(8,128)(2,1)S(1)} %slice.18), channel_id=1, source_target_pairs={{0,64},{64,128},{128,192},{192,256},{256,320},{320,384},{384,448},... | collective-permute-start | bytes 884744 | tf_op jit(solution)/shard_map/ppermute | solution.py:131
  105.3 11.2 %copy-start.14 = (bf16[264,1152]{1,0:T(8,128)(2,1)}, bf16[264,1152]{1,0:T(8,128)(2,1)S(1)}, u32[]{:S(2)}) copy-start(bf16[264,1152]{1,0:T(8,128)(2,1)S(1)} %collective-permute-done.14.refs_16_) | copy-start | bytes 1824772
  105.3 11.2 %collective-permute-start.6 = (bf16[128,1024]{1,0:T(8,128)(2,1)S(1)}, bf16[128,1024]{1,0:T(8,128)(2,1)S(1)}, u32[]{:S(2)}, u32[]{:S(2)}) collective-permute-start(bf16[128,1024]{1,0:T(8,128)(2,1)S(1)} %slice.16), channel_id=1, source_target_pairs={{0,8},{8,16},{16,24},{24,32},{32,40},{40,48},{48,56},{56,0},{1,9},... | collective-permute-start | bytes 786440 | tf_op jit(solution)/shard_map/ppermute | solution.py:133
  107.3 19.6 %copy-start.19 = (bf16[136,1152]{1,0:T(8,128)(2,1)}, bf16[136,1152]{1,0:T(8,128)(2,1)S(1)}, u32[]{:S(2)}) copy-start(bf16[136,1152]{1,0:T(8,128)(2,1)S(1)} %collective-permute-done.23.refs_25_) | copy-start | bytes 940036
  107.3 19.6 %collective-permute-start.24 = (bf16[136,1152]{1,0:T(8,128)(2,1)S(1)}, bf16[136,1152]{1,0:T(8,128)(2,1)}, u32[]{:S(2)}, u32[]{:S(2)}) collective-permute-start(bf16[136,1152]{1,0:T(8,128)(2,1)S(1)} %collective-permute-done.23.refs_25_), channel_id=1, source_target_pairs={{0,4},{4,0},{1,5},{5,1},{2,6},{6,2},{3,7},{7,3},{8,12},{12,8},{9,1... | collective-permute-start | bytes 940040 | tf_op jit(solution)/shard_map/ppermute | solution.py:114
  113.2 13.6 %collective-permute-start.22 = (bf16[128,1152]{1,0:T(8,128)(2,1)}, bf16[128,1152]{1,0:T(8,128)(2,1)}, u32[]{:S(2)}, u32[]{:S(2)}) collective-permute-start(bf16[128,1152]{1,0:T(8,128)(2,1)} %collective-permute-done.21.refs_23_), channel_id=1, source_target_pairs={{0,4},{4,0},{1,5},{5,1},{2,6},{6,2},{3,7},{7,3},{8,12},{12,8},{9,1... | collective-permute-start | bytes 884744 | tf_op jit(solution)/shard_map/ppermute | solution.py:114
  116.6 0.7 copy-start.20
  117.3 9.6 %collective-permute-start.7 = (bf16[136,1024]{1,0:T(8,128)(2,1)S(1)}, bf16[136,1024]{1,0:T(8,128)(2,1)}, u32[]{:S(2)}, u32[]{:S(2)}) collective-permute-start(bf16[136,1024]{1,0:T(8,128)(2,1)S(1)} %slice.17), channel_id=1, source_target_pairs={{0,56},{8,0},{16,8},{24,16},{32,24},{40,32},{48,40},{56,48},{1,57}... | collective-permute-start | bytes 835592 | tf_op jit(solution)/shard_map/ppermute | solution.py:134
  165.7 6.2 %collective-permute-start.25 = (f32[1,4096]{1,0:T(1,128)}, f32[1,4096]{1,0:T(1,128)S(1)}, u32[]{:S(2)}, u32[]{:S(2)}) collective-permute-start(f32[1,4096]{1,0:T(1,128)} %get-tuple-element.10), channel_id=1, source_target_pairs={{0,2},{2,0},{1,3},{3,1},{4,6},{6,4},{5,7},{7,5},{8,10},{10,8},{9,1... | collective-permute-start | bytes 49160 | tf_op jit(solution)/shard_map/ppermute | solution.py:349
  202.6 20.9 %all-to-all-start.1 = ((bf16[16,128,128]{2,1,0:T(8,128)(2,1)}), bf16[16,128,128]{2,1,0:T(8,128)(2,1)S(1)}, u32[]{:S(2)}, u32[]{:S(2)}) async-start(bf16[16,128,128]{2,1,0:T(8,128)(2,1)} %bitcast.10), calls=%async_computation.1 | async-start | bytes 1048576 | tf_op jit(solution)/shard_map/all_to_all | solution.py:357
  377.4 14.5 %all-to-all-start.7 = ((f32[4,128,128]{2,1,0:T(8,128)}), f32[4,128,128]{2,1,0:T(8,128)S(1)}, u32[]{:S(2)}, u32[]{:S(2)}) async-start(f32[4,128,128]{2,1,0:T(8,128)} %broadcast_in_dim.26), calls=%async_computation.7 | async-start | bytes 524288 | tf_op jit(solution)/shard_map/all_to_all | solution.py:25
where the time goes:
time: 396 us; the launch traced here: 394 us
  blocking collectives  150 us (38%)
  starting transfers between devices  95.9 us (24%)
  Pallas kernels  60.9 us (15%)
  waiting for transfers between devices  56.5 us (14%)
  matrix products  23.3 us (6%)
  local copies, waits for them, and re-layouts  4.65 us (1%)
    all_to_all x6, blocking collectives, from_everyone(): return lax.all_to_all(copies, axes, split_axis=0, concat_axis=0, tiled=True)  99.5 us
    pallas_call x1, Pallas kernels, build_tile(): pl.pallas_call(kernel, out_shape=(jax.ShapeDtypeStruct((height, width), j...  38.8 us
    all_to_all x2, blocking collectives, gram_total(): lax.all_to_all(parts, wide, split_axis=0, concat_axis=0, tiled=True)  31.7 us
    ppermute x9, starting transfers between devices, keep(): other = lax.ppermute(piece, 'c', [(0, 1), (1, 0)])  26.1 us
    pallas_call x2, Pallas kernels, inverse_factor(): pl.pallas_call(inverse_factor_kernel, out_shape=jax.ShapeDtypeStruct(gram...  22.1 us
    ppermute x3, waiting for transfers between devices, exchange(): row_a = lax.ppermute(row_a, 'z', onward)  20.5 us
    ppermute x3, starting transfers between devices, exchange(): row_b = lax.ppermute(row_b, 'z', backward)  20.4 us
    dot_general x2, matrix products, on_device(): jnp.dot(tile, fetched, preferred_element_type=jnp.float32)  19.6 us
  transfers between devices with their start and end apart: 28, of which 8 were waited for; matrix products, arithmetic and copies ran while one was open for 0% of the time, Pallas kernels for 3%

commit v1 on v0

--- a/solution.py
+++ b/solution.py
@@ -146,12 +146,13 @@
     rows_v, cols_v, start_v, row_links, col_links, weight, w_v, sems, out_sems = refs[count + 3 :]
     y, z, c, xa, xb = (ids[i] for i in range(5))
     row_owners, col_owners = z_count, 2 * y_count
-    copies = []
+    copies, notes = [], []
 
     def copy(src, dst):
         made = pltpu.make_async_copy(src, dst, sems.at[len(copies)])
         made.start()
         copies.append(made)
+        return made
 
     for slot, source, k, first, height in row_plan:
         ref = pieces[slot]
@@ -160,7 +161,7 @@
         at = pl.multiple_of(owner * PAIR + first, BLOCK)
         copy(ref.at[pl.ds(source, body)], rows_v.at[pl.ds(at, body)])
         if first + height > PAIR:
-            copy(ref.at[pl.ds(source + body, EXTRA), pl.ds(0, BLOCK)], row_links.at[owner])
+            notes.append(copy(ref.at[pl.ds(source + body, EXTRA), pl.ds(0, BLOCK)], row_links.at[owner]))
     for slot, source, k, first, other, height in col_plan:
         ref = pieces[slot]
         owner = lax.rem(y + k, y_count) * 2 + (1 - c if other else c)
@@ -170,11 +171,9 @@
         copy(ref.at[from_rows, pl.ds(0, features)], cols_v.at[pl.ds(at, body)])
         copy(ref.at[from_rows, pl.ds(features, comps)], start_v.at[pl.ds(at, body)])
         if first + height > PAIR:
-            copy(ref.at[pl.ds(source + body, EXTRA), pl.ds(0, BLOCK)], col_links.at[owner])
-    for made in copies:
+            notes.append(copy(ref.at[pl.ds(source + body, EXTRA), pl.ds(0, BLOCK)], col_links.at[owner]))
+    for made in notes:
         made.wait()
-    v_copy = pltpu.make_async_copy(start_v, v_out, out_sems.at[col_owners])
-    v_copy.start()
 
     width = col_owners * PAIR
     lane = lax.broadcasted_iota(jnp.int32, (BLOCK, width), 1)
@@ -199,6 +198,11 @@
         row_block = (2 * xa + half).astype(jnp.float32)
         weight[half] = base + (back == row_block).astype(jnp.float32)
 
+    for made in copies:
+        if not any(made is note for note in notes):
+            made.wait()
+    v_copy = pltpu.make_async_copy(start_v, v_out, out_sems.at[col_owners])
+    v_copy.start()
     factor = 2.0 / math.sqrt(features) * math.log2(math.e)
 
     def scale_of(values):

time: 396 us -> 396 us (level)
  no operation moved by 1% of the time
where the time goes in v1:
time: 396 us; the launch traced here: 394 us
  blocking collectives  150 us (38%)
  starting transfers between devices  95.9 us (24%)
  Pallas kernels  61.2 us (15%)
  waiting for transfers between devices  56.5 us (14%)
  matrix products  23.3 us (6%)
  local copies, waits for them, and re-layouts  4.65 us (1%)
    all_to_all x6, blocking collectives, from_everyone(): return lax.all_to_all(copies, axes, split_axis=0, concat_axis=0, tiled=True)  99.5 us
    pallas_call x1, Pallas kernels, build_tile(): pl.pallas_call(kernel, out_shape=(jax.ShapeDtypeStruct((height, width), j...  39.1 us
    all_to_all x2, blocking collectives, gram_total(): lax.all_to_all(parts, wide, split_axis=0, concat_axis=0, tiled=True)  31.7 us
    ppermute x9, starting transfers between devices, keep(): other = lax.ppermute(piece, 'c', [(0, 1), (1, 0)])  26.1 us
    pallas_call x2, Pallas kernels, inverse_factor(): pl.pallas_call(inverse_factor_kernel, out_shape=jax.ShapeDtypeStruct(gram...  22.1 us
    ppermute x3, waiting for transfers between devices, exchange(): row_a = lax.ppermute(row_a, 'z', onward)  20.5 us
    ppermute x3, starting transfers between devices, exchange(): row_b = lax.ppermute(row_b, 'z', backward)  20.4 us
    dot_general x2, matrix products, on_device(): jnp.dot(tile, fetched, preferred_element_type=jnp.float32)  19.6 us
  transfers between devices with their start and end apart: 28, of which 8 were waited for; matrix products, arithmetic and copies ran while one was open for 0% of the time, Pallas kernels for 3%

profile of v1, /device:TPU:1, one launch (start us, length us, event | category | flops | bytes accessed | tf_op | source)
XLA Modules:
  0.0 394.1 jit_solution(13741935206308178041)
XLA Ops:
  0.0 0.7 convert_element_type.30
  0.8 0.8 constant_dynamic-slice_fusion
  1.7 5.9 %collective-permute-start.11 = (bf16[264,1152]{1,0:T(8,128)(2,1)S(1)}, bf16[264,1152]{1,0:T(8,128)(2,1)S(1)}, u32[]{:S(2)}, u32[]{:S(2)}) collective-permute-start(bf16[264,1152]{1,0:T(8,128)(2,1)S(1)} %fusion.4.refs_9_), channel_id=1, source_target_pairs={{0,448},{64,0},{128,64},{192,128},{256,192},{320,256},{384,320},{4... | collective-permute-start | bytes 1824776 | tf_op jit(solution)/shard_map/ppermute | solution.py:123
  7.7 10.7 %collective-permute-start.1 = (bf16[264,1024]{1,0:T(8,128)(2,1)S(1)}, bf16[264,1024]{1,0:T(8,128)(2,1)S(1)}, u32[]{:S(2)}, u32[]{:S(2)}) collective-permute-start(bf16[264,1024]{1,0:T(8,128)(2,1)S(1)} %fusion.5.refs_0_), channel_id=1, source_target_pairs={{0,56},{8,0},{16,8},{24,16},{32,24},{40,32},{48,40},{56,48},{1,57}... | collective-permute-start | bytes 1622024 | tf_op jit(solution)/shard_map/ppermute | solution.py:125
  18.4 1.9 collective-permute-start.9
  20.4 3.1 collective-permute-start.8
  23.5 4.9 %collective-permute-start.15 = (bf16[264,1152]{1,0:T(8,128)(2,1)S(1)}, bf16[264,1152]{1,0:T(8,128)(2,1)S(1)}, u32[]{:S(2)}, u32[]{:S(2)}) collective-permute-start(bf16[264,1152]{1,0:T(8,128)(2,1)S(1)} %collective-permute-done.11.refs_13_), channel_id=1, source_target_pairs={{0,448},{64,0},{128,64},{192,128},{256,192},{320,256},{384,320},{4... | collective-permute-start | bytes 1824776 | tf_op jit(solution)/shard_map/ppermute | solution.py:123
  28.4 1.9 collective-permute-start
  30.3 7.6 %collective-permute-start.3 = (bf16[264,1024]{1,0:T(8,128)(2,1)S(1)}, bf16[264,1024]{1,0:T(8,128)(2,1)S(1)}, u32[]{:S(2)}, u32[]{:S(2)}) collective-permute-start(bf16[264,1024]{1,0:T(8,128)(2,1)S(1)} %collective-permute-done.1.refs_2_), channel_id=1, source_target_pairs={{0,56},{8,0},{16,8},{24,16},{32,24},{40,32},{48,40},{56,48},{1,57}... | collective-permute-start | bytes 1622024 | tf_op jit(solution)/shard_map/ppermute | solution.py:125
  38.0 1.9 collective-permute-start.13
  39.9 6.9 %collective-permute-done.refs_1_ = bf16[264,1024]{1,0:T(8,128)(2,1)S(1)} collective-permute-done((bf16[264,1024]{1,0:T(8,128)(2,1)S(1)}, bf16[264,1024]{1,0:T(8,128)(2,1)S(1)}, u32[]{:S(2)}, u32[]{:S(2)}) %collective-permute-start) | collective-permute-done | bytes 540704 | tf_op jit(solution)/shard_map/ppermute | solution.py:124
  46.8 4.3 %collective-permute-start.12 = (bf16[264,1152]{1,0:T(8,128)(2,1)S(1)}, bf16[264,1152]{1,0:T(8,128)(2,1)S(1)}, u32[]{:S(2)}, u32[]{:S(2)}) collective-permute-start(bf16[264,1152]{1,0:T(8,128)(2,1)S(1)} %collective-permute-done.11.refs_13_), channel_id=1, source_target_pairs={{0,4},{4,0},{1,5},{5,1},{2,6},{6,2},{3,7},{7,3},{8,12},{12,8},{9,1... | collective-permute-start | bytes 1824776 | tf_op jit(solution)/shard_map/ppermute | solution.py:114
  51.2 1.9 collective-permute-start.10
  53.1 1.9 collective-permute-start.19
  55.1 1.9 collective-permute-start.2
  57.0 3.4 collective-permute-start.17
  60.4 10.9 %collective-permute-done.2.refs_3_ = bf16[264,1024]{1,0:T(8,128)(2,1)S(1)} collective-permute-done((bf16[264,1024]{1,0:T(8,128)(2,1)S(1)}, bf16[264,1024]{1,0:T(8,128)(2,1)S(1)}, u32[]{:S(2)}, u32[]{:S(2)}) %collective-permute-start.2) | collective-permute-done | bytes 540704 | tf_op jit(solution)/shard_map/ppermute | solution.py:124
  71.3 3.4 collective-permute-start.16
  74.8 2.2 collective-permute-start.5
  77.0 2.2 collective-permute-start.14
  79.3 3.1 collective-permute-start.4
  82.4 8.1 %collective-permute-done.5.refs_6_ = bf16[264,1024]{1,0:T(8,128)(2,1)S(1)} collective-permute-done((bf16[264,1024]{1,0:T(8,128)(2,1)S(1)}, bf16[264,1024]{1,0:T(8,128)(2,1)S(1)}, u32[]{:S(2)}, u32[]{:S(2)}) %collective-permute-start.5) | collective-permute-done | bytes 540704 | tf_op jit(solution)/shard_map/ppermute | solution.py:125
  90.5 2.8 collective-permute-start.23
  93.3 2.6 collective-permute-done.4.refs_5_
  96.0 3.0 collective-permute-start.20
  99.0 1.9 collective-permute-start.18
  100.9 1.0 slice.18
  101.9 3.4 collective-permute-start.21
  105.3 1.9 collective-permute-start.6
  107.3 3.0 collective-permute-start.24
  110.3 2.9 collective-permute-done.21.refs_23_
  113.2 3.3 collective-permute-start.22
  116.6 0.7 copy-done.20
  117.3 1.9 collective-permute-start.7
  119.2 0.6 stack.23.ids
  119.8 7.0 %collective-permute-done.7.refs_8_ = bf16[136,1024]{1,0:T(8,128)(2,1)} collective-permute-done((bf16[136,1024]{1,0:T(8,128)(2,1)S(1)}, bf16[136,1024]{1,0:T(8,128)(2,1)}, u32[]{:S(2)}, u32[]{:S(2)}) %collective-permute-start.7) | collective-permute-done | bytes 278560 | tf_op jit(solution)/shard_map/ppermute | solution.py:134
  126.9 39.1 %affinity_tile.1 = (bf16[2048,4096]{1,0:T(8,128)(2,1)}, f32[1,4096]{1,0:T(1,128)}, bf16[4096,128]{1,0:T(8,128)(2,1)}) custom-call(s32[5]{0:T(128)} %stack.23.ids, bf16[264,1024]{1,0:T(8,128)(2,1)} %copy-done.2, bf16[264,1024]{1,0:T(8,128)(2,1)} %copy-done.16, bf16[264,1024]{1,0:T(8,128)(2,1)} %copy-done.15, bf16[264,1024]{1,0:T(8,128)(2,1)} %copy-done.18, ...), custom_call_target="tpu_custom_call" | custom-call | flops 17179869184 | bytes 29360128 | tf_op jit(solution)/shard_map/affinity_tile/pallas_call | solution.py:292
  166.0 4.6 %collective-permute-start.25 = (f32[1,4096]{1,0:T(1,128)}, f32[1,4096]{1,0:T(1,128)S(1)}, u32[]{:S(2)}, u32[]{:S(2)}) collective-permute-start(f32[1,4096]{1,0:T(1,128)} %get-tuple-element.10), channel_id=1, source_target_pairs={{0,2},{2,0},{1,3},{3,1},{4,6},{6,4},{5,7},{7,5},{8,10},{10,8},{9,1... | collective-permute-start | bytes 49160 | tf_op jit(solution)/shard_map/ppermute | solution.py:353
  170.6 1.5 collective-permute-done.25
  172.2 0.7 add.31
  172.9 0.2 broadcast_in_dim.22
  173.1 18.1 %all_to_all.55 = f32[16,1,4096]{2,1,0:T(1,128)S(1)} all-to-all(f32[16,1,4096]{2,1,0:T(1,128)S(1)} %broadcast_in_dim.22), channel_id=1, replica_groups=mesh['y'=8,'z'=8,'c'=2,'xa'=2,'xb'=2] {'y','c'}, dimensions={0} | all-to-all | bytes 524288 | tf_op jit(solution)/shard_map/all_to_all | solution.py:25
  191.3 0.2 reduce_sum.63
  191.4 11.5 %convolution_convert_fusion.1 = bf16[2048,128]{1,0:T(8,128)(2,1)} fusion(bf16[2048,4096]{1,0:T(8,128)(2,1)} %get-tuple-element.8, bf16[4096,128]{1,0:T(8,128)(2,1)} %get-tuple-element.9, f32[4096]{0:T(1024)S(1)} %rsqrt.16), kind=kOutput, calls=%fused_computation.1 | convolution fusion | flops 2149318656 | bytes 18366464 | tf_op jit(solution)/shard_map/dot_general | solution.py:359
  202.9 4.5 %all-to-all-start.1 = ((bf16[16,128,128]{2,1,0:T(8,128)(2,1)}), bf16[16,128,128]{2,1,0:T(8,128)(2,1)S(1)}, u32[]{:S(2)}, u32[]{:S(2)}) async-start(bf16[16,128,128]{2,1,0:T(8,128)(2,1)} %bitcast.10), calls=%async_computation.1 | async-start | bytes 1048576 | tf_op jit(solution)/shard_map/all_to_all | solution.py:361
  207.5 16.4 %all-to-all-done.1 = bf16[16,128,128]{2,1,0:T(8,128)(2,1)S(1)} async-done(((bf16[16,128,128]{2,1,0:T(8,128)(2,1)}), bf16[16,128,128]{2,1,0:T(8,128)(2,1)S(1)}, u32[]{:S(2)}, u32[]{:S(2)}) %all-to-all-start.1) | async-done | bytes 524320 | tf_op jit(solution)/shard_map/all_to_all | solution.py:361
  223.9 0.4 fusion.7
  224.3 15.1 %all_to_all.56 = f32[32,4,128]{2,1,0:T(4,128)S(1)} all-to-all(f32[32,4,128]{2,1,0:T(4,128)S(1)} %bitcast.39), channel_id=1, replica_groups=mesh['y'=8,'z'=8,'c'=2,'xa'=2,'xb'=2] {'z','xa','xb'}, dimensions={0} | all-to-all | bytes 131072 | tf_op jit(solution)/shard_map/all_to_all | solution.py:35
  239.5 11.8 %all_to_all.57 = f32[16,4,128]{2,1,0:T(4,128)S(1)} all-to-all(f32[16,4,128]{2,1,0:T(4,128)S(1)} %broadcast_in_dim.23), channel_id=1, replica_groups=mesh['y'=8,'z'=8,'c'=2,'xa'=2,'xb'=2] {'y','c'}, dimensions={0} | all-to-all | bytes 65536 | tf_op jit(solution)/shard_map/all_to_all | solution.py:25
  251.3 12.5 %all_to_all.58 = f32[32,4,128]{2,1,0:T(4,128)} all-to-all(f32[32,4,128]{2,1,0:T(4,128)S(1)} %broadcast_in_dim.24), channel_id=1, replica_groups=mesh['y'=8,'z'=8,'c'=2,'xa'=2,'xb'=2] {'z','xa','xb'}, dimensions={0} | all-to-all | bytes 131072 | tf_op jit(solution)/shard_map/all_to_all | solution.py:25
  263.8 11.1 %inverse_factor.2 = f32[128,128]{1,0:T(8,128)} custom-call(f32[128,128]{1,0:T(8,128)} %bitcast.38), custom_call_target="tpu_custom_call" | custom-call | tf_op jit(solution)/shard_map/inverse_factor/pallas_call | solution.py:88
  274.9 1.1 fusion.1
  276.0 0.2 broadcast_in_dim.25
  276.3 32.7 %all_to_all.59 = bf16[32,128,128]{2,1,0:T(8,128)(2,1)S(1)} all-to-all(bf16[32,128,128]{2,1,0:T(8,128)(2,1)S(1)} %broadcast_in_dim.25), channel_id=1, replica_groups=mesh['y'=8,'z'=8,'c'=2,'xa'=2,'xb'=2] {'y','c','xa'}, dimensions={0} | all-to-all | bytes 2097152 | tf_op jit(solution)/shard_map/all_to_all | solution.py:25
  309.0 8.2 %convolution_convert_fusion = bf16[2048,128]{1,0:T(8,128)(2,1)S(1)} fusion(bf16[2048,4096]{1,0:T(8,128)(2,1)} %get-tuple-element.8, bf16[4096,128]{1,0:T(8,128)(2,1)S(1)} %bitcast.32), kind=kOutput, calls=%fused_computation | convolution fusion | flops 2147745792 | bytes 18350080 | tf_op jit(solution)/shard_map/dot_general | solution.py:359
  317.2 18.3 %all_to_all.60 = bf16[16,128,128]{2,1,0:T(8,128)(2,1)S(1)} all-to-all(bf16[16,128,128]{2,1,0:T(8,128)(2,1)S(1)} %bitcast.34), channel_id=1, replica_groups=mesh['y'=8,'z'=8,'c'=2,'xa'=2,'xb'=2] {'z','xb'}, dimensions={0} | all-to-all | bytes 1048576 | tf_op jit(solution)/shard_map/all_to_all | solution.py:361
  335.6 0.3 fusion.11
  335.9 16.6 %all_to_all.61 = f32[32,4,128]{2,1,0:T(4,128)S(1)} all-to-all(f32[32,4,128]{2,1,0:T(4,128)S(1)} %bitcast.36), channel_id=1, replica_groups=mesh['y'=8,'z'=8,'c'=2,'xa'=2,'xb'=2] {'z','xa','xb'}, dimensions={0} | all-to-all | bytes 131072 | tf_op jit(solution)/shard_map/all_to_all | solution.py:35
  352.6 11.8 %all_to_all.62 = f32[16,4,128]{2,1,0:T(4,128)S(1)} all-to-all(f32[16,4,128]{2,1,0:T(4,128)S(1)} %broadcast_in_dim.27), channel_id=1, replica_groups=mesh['y'=8,'z'=8,'c'=2,'xa'=2,'xb'=2] {'y','c'}, dimensions={0} | all-to-all | bytes 65536 | tf_op jit(solution)/shard_map/all_to_all | solution.py:25
  364.5 12.5 %all_to_all.63 = f32[32,4,128]{2,1,0:T(4,128)} all-to-all(f32[32,4,128]{2,1,0:T(4,128)S(1)} %broadcast_in_dim.28), channel_id=1, replica_groups=mesh['y'=8,'z'=8,'c'=2,'xa'=2,'xb'=2] {'z','xa','xb'}, dimensions={0} | all-to-all | bytes 131072 | tf_op jit(solution)/shard_map/all_to_all | solution.py:25
  377.0 0.7 broadcast_in_dim.26
  377.7 3.4 all-to-all-start.7
  381.1 11.1 %inverse_factor.3 = f32[128,128]{1,0:T(8,128)} custom-call(f32[128,128]{1,0:T(8,128)} %bitcast.37), custom_call_target="tpu_custom_call" | custom-call | tf_op jit(solution)/shard_map/inverse_factor/pallas_call | solution.py:88
  392.2 1.9 convolution_multiply_fusion
  (82 shorter events, 0.9 us)
Async XLA Ops:
  0.0 1.6 copy-start
  1.7 80.7 %copy-start.1 = (bf16[264,1152]{1,0:T(8,128)(2,1)}, bf16[264,1152]{1,0:T(8,128)(2,1)S(1)}, u32[]{:S(2)}) copy-start(bf16[264,1152]{1,0:T(8,128)(2,1)S(1)} %fusion.4.refs_9_) | copy-start | bytes 1824772
  1.7 21.8 %collective-permute-start.11 = (bf16[264,1152]{1,0:T(8,128)(2,1)S(1)}, bf16[264,1152]{1,0:T(8,128)(2,1)S(1)}, u32[]{:S(2)}, u32[]{:S(2)}) collective-permute-start(bf16[264,1152]{1,0:T(8,128)(2,1)S(1)} %fusion.4.refs_9_), channel_id=1, source_target_pairs={{0,448},{64,0},{128,64},{192,128},{256,192},{320,256},{384,320},{4... | collective-permute-start | bytes 1824776 | tf_op jit(solution)/shard_map/ppermute | solution.py:123
  7.7 119.1 %copy-start.2 = (bf16[264,1024]{1,0:T(8,128)(2,1)}, bf16[264,1024]{1,0:T(8,128)(2,1)S(1)}, u32[]{:S(2)}) copy-start(bf16[264,1024]{1,0:T(8,128)(2,1)S(1)} %fusion.5.refs_0_) | copy-start | bytes 1622020
  7.7 22.6 %collective-permute-start.1 = (bf16[264,1024]{1,0:T(8,128)(2,1)S(1)}, bf16[264,1024]{1,0:T(8,128)(2,1)S(1)}, u32[]{:S(2)}, u32[]{:S(2)}) collective-permute-start(bf16[264,1024]{1,0:T(8,128)(2,1)S(1)} %fusion.5.refs_0_), channel_id=1, source_target_pairs={{0,56},{8,0},{16,8},{24,16},{32,24},{40,32},{48,40},{56,48},{1,57}... | collective-permute-start | bytes 1622024 | tf_op jit(solution)/shard_map/ppermute | solution.py:125
  18.4 19.5 %collective-permute-start.9 = (bf16[264,1152]{1,0:T(8,128)(2,1)S(1)}, bf16[264,1152]{1,0:T(8,128)(2,1)S(1)}, u32[]{:S(2)}, u32[]{:S(2)}) collective-permute-start(bf16[264,1152]{1,0:T(8,128)(2,1)S(1)} %fusion.4.refs_9_), channel_id=1, source_target_pairs={{0,64},{64,128},{128,192},{192,256},{256,320},{320,384},{384,448},... | collective-permute-start | bytes 1824776 | tf_op jit(solution)/shard_map/ppermute | solution.py:122
  20.4 30.8 %collective-permute-start.8 = (bf16[264,1152]{1,0:T(8,128)(2,1)S(1)}, bf16[264,1152]{1,0:T(8,128)(2,1)S(1)}, u32[]{:S(2)}, u32[]{:S(2)}) collective-permute-start(bf16[264,1152]{1,0:T(8,128)(2,1)S(1)} %fusion.4.refs_9_), channel_id=1, source_target_pairs={{0,4},{4,0},{1,5},{5,1},{2,6},{6,2},{3,7},{7,3},{8,12},{12,8},{9,1... | collective-permute-start | bytes 1824776 | tf_op jit(solution)/shard_map/ppermute | solution.py:114
  23.5 51.3 %copy-start.6 = (bf16[264,1152]{1,0:T(8,128)(2,1)}, bf16[264,1152]{1,0:T(8,128)(2,1)S(1)}, u32[]{:S(2)}) copy-start(bf16[264,1152]{1,0:T(8,128)(2,1)S(1)} %collective-permute-done.11.refs_13_) | copy-start | bytes 1824772
  23.5 29.6 %collective-permute-start.15 = (bf16[264,1152]{1,0:T(8,128)(2,1)S(1)}, bf16[264,1152]{1,0:T(8,128)(2,1)S(1)}, u32[]{:S(2)}, u32[]{:S(2)}) collective-permute-start(bf16[264,1152]{1,0:T(8,128)(2,1)S(1)} %collective-permute-done.11.refs_13_), channel_id=1, source_target_pairs={{0,448},{64,0},{128,64},{192,128},{256,192},{320,256},{384,320},{4... | collective-permute-start | bytes 1824776 | tf_op jit(solution)/shard_map/ppermute | solution.py:123
  28.4 18.5 %collective-permute-start = (bf16[264,1024]{1,0:T(8,128)(2,1)S(1)}, bf16[264,1024]{1,0:T(8,128)(2,1)S(1)}, u32[]{:S(2)}, u32[]{:S(2)}) collective-permute-start(bf16[264,1024]{1,0:T(8,128)(2,1)S(1)} %fusion.5.refs_0_), channel_id=1, source_target_pairs={{0,8},{8,16},{16,24},{24,32},{32,40},{40,48},{48,56},{56,0},{1,9},... | collective-permute-start | bytes 1622024 | tf_op jit(solution)/shard_map/ppermute | solution.py:124
  30.3 48.9 %copy-start.15 = (bf16[264,1024]{1,0:T(8,128)(2,1)}, bf16[264,1024]{1,0:T(8,128)(2,1)S(1)}, u32[]{:S(2)}) copy-start(bf16[264,1024]{1,0:T(8,128)(2,1)S(1)} %collective-permute-done.1.refs_2_) | copy-start | bytes 1622020
  30.3 24.7 %collective-permute-start.3 = (bf16[264,1024]{1,0:T(8,128)(2,1)S(1)}, bf16[264,1024]{1,0:T(8,128)(2,1)S(1)}, u32[]{:S(2)}, u32[]{:S(2)}) collective-permute-start(bf16[264,1024]{1,0:T(8,128)(2,1)S(1)} %collective-permute-done.1.refs_2_), channel_id=1, source_target_pairs={{0,56},{8,0},{16,8},{24,16},{32,24},{40,32},{48,40},{56,48},{1,57}... | collective-permute-start | bytes 1622024 | tf_op jit(solution)/shard_map/ppermute | solution.py:125
  38.0 41.2 %copy-start.7 = (bf16[264,1152]{1,0:T(8,128)(2,1)}, bf16[264,1152]{1,0:T(8,128)(2,1)S(1)}, u32[]{:S(2)}) copy-start(bf16[264,1152]{1,0:T(8,128)(2,1)S(1)} %collective-permute-done.9.refs_11_) | copy-start | bytes 1824772
  38.0 19.0 %collective-permute-start.13 = (bf16[264,1152]{1,0:T(8,128)(2,1)S(1)}, bf16[264,1152]{1,0:T(8,128)(2,1)S(1)}, u32[]{:S(2)}, u32[]{:S(2)}) collective-permute-start(bf16[264,1152]{1,0:T(8,128)(2,1)S(1)} %collective-permute-done.9.refs_11_), channel_id=1, source_target_pairs={{0,64},{64,128},{128,192},{192,256},{256,320},{320,384},{384,448},... | collective-permute-start | bytes 1824776 | tf_op jit(solution)/shard_map/ppermute | solution.py:122
  46.8 32.4 %copy-start.16 = (bf16[264,1024]{1,0:T(8,128)(2,1)}, bf16[264,1024]{1,0:T(8,128)(2,1)S(1)}, u32[]{:S(2)}) copy-start(bf16[264,1024]{1,0:T(8,128)(2,1)S(1)} %collective-permute-done.refs_1_) | copy-start | bytes 1622020
  46.8 27.9 %collective-permute-start.12 = (bf16[264,1152]{1,0:T(8,128)(2,1)S(1)}, bf16[264,1152]{1,0:T(8,128)(2,1)S(1)}, u32[]{:S(2)}, u32[]{:S(2)}) collective-permute-start(bf16[264,1152]{1,0:T(8,128)(2,1)S(1)} %collective-permute-done.11.refs_13_), channel_id=1, source_target_pairs={{0,4},{4,0},{1,5},{5,1},{2,6},{6,2},{3,7},{7,3},{8,12},{12,8},{9,1... | collective-permute-start | bytes 1824776 | tf_op jit(solution)/shard_map/ppermute | solution.py:114
  51.1 1.9 copy-start.8
  51.2 25.8 %collective-permute-start.10 = (bf16[264,1152]{1,0:T(8,128)(2,1)S(1)}, bf16[264,1152]{1,0:T(8,128)(2,1)S(1)}, u32[]{:S(2)}, u32[]{:S(2)}) collective-permute-start(bf16[264,1152]{1,0:T(8,128)(2,1)S(1)} %collective-permute-done.9.refs_11_), channel_id=1, source_target_pairs={{0,4},{4,0},{1,5},{5,1},{2,6},{6,2},{3,7},{7,3},{8,12},{12,8},{9,1... | collective-permute-start | bytes 1824776 | tf_op jit(solution)/shard_map/ppermute | solution.py:114
  53.1 63.4 %copy-start.9 = (bf16[264,1152]{1,0:T(8,128)(2,1)}, bf16[264,1152]{1,0:T(8,128)(2,1)S(1)}, u32[]{:S(2)}) copy-start(bf16[264,1152]{1,0:T(8,128)(2,1)S(1)} %collective-permute-done.15.refs_17_) | copy-start | bytes 1824772
  53.1 26.1 %collective-permute-start.19 = (bf16[264,1152]{1,0:T(8,128)(2,1)S(1)}, bf16[264,1152]{1,0:T(8,128)(2,1)S(1)}, u32[]{:S(2)}, u32[]{:S(2)}) collective-permute-start(bf16[264,1152]{1,0:T(8,128)(2,1)S(1)} %collective-permute-done.15.refs_17_), channel_id=1, source_target_pairs={{0,448},{64,0},{128,64},{192,128},{256,192},{320,256},{384,320},{4... | collective-permute-start | bytes 1824776 | tf_op jit(solution)/shard_map/ppermute | solution.py:123
  55.1 43.9 %copy-start.17 = (bf16[264,1024]{1,0:T(8,128)(2,1)}, bf16[264,1024]{1,0:T(8,128)(2,1)S(1)}, u32[]{:S(2)}) copy-start(bf16[264,1024]{1,0:T(8,128)(2,1)S(1)} %collective-permute-done.3.refs_4_) | copy-start | bytes 1622020
  55.1 16.3 %collective-permute-start.2 = (bf16[264,1024]{1,0:T(8,128)(2,1)S(1)}, bf16[264,1024]{1,0:T(8,128)(2,1)S(1)}, u32[]{:S(2)}, u32[]{:S(2)}) collective-permute-start(bf16[264,1024]{1,0:T(8,128)(2,1)S(1)} %collective-permute-done.refs_1_), channel_id=1, source_target_pairs={{0,8},{8,16},{16,24},{24,32},{32,40},{40,48},{48,56},{56,0},{1,9},... | collective-permute-start | bytes 1622024 | tf_op jit(solution)/shard_map/ppermute | solution.py:124
  57.0 59.5 %copy-start.10 = (bf16[264,1152]{1,0:T(8,128)(2,1)}, bf16[264,1152]{1,0:T(8,128)(2,1)S(1)}, u32[]{:S(2)}) copy-start(bf16[264,1152]{1,0:T(8,128)(2,1)S(1)} %collective-permute-done.13.refs_15_) | copy-start | bytes 1824772
  57.0 41.9 %collective-permute-start.17 = (bf16[264,1152]{1,0:T(8,128)(2,1)S(1)}, bf16[264,1152]{1,0:T(8,128)(2,1)}, u32[]{:S(2)}, u32[]{:S(2)}) collective-permute-start(bf16[264,1152]{1,0:T(8,128)(2,1)S(1)} %collective-permute-done.13.refs_15_), channel_id=1, source_target_pairs={{0,64},{64,128},{128,192},{192,256},{256,320},{320,384},{384,448},... | collective-permute-start | bytes 1824776 | tf_op jit(solution)/shard_map/ppermute | solution.py:122
  71.3 45.2 %copy-start.18 = (bf16[264,1024]{1,0:T(8,128)(2,1)}, bf16[264,1024]{1,0:T(8,128)(2,1)S(1)}, u32[]{:S(2)}) copy-start(bf16[264,1024]{1,0:T(8,128)(2,1)S(1)} %collective-permute-done.2.refs_3_) | copy-start | bytes 1622020
  71.3 30.6 %collective-permute-start.16 = (bf16[264,1152]{1,0:T(8,128)(2,1)S(1)}, bf16[264,1152]{1,0:T(8,128)(2,1)S(1)}, u32[]{:S(2)}, u32[]{:S(2)}) collective-permute-start(bf16[264,1152]{1,0:T(8,128)(2,1)S(1)} %collective-permute-done.15.refs_17_), channel_id=1, source_target_pairs={{0,4},{4,0},{1,5},{5,1},{2,6},{6,2},{3,7},{7,3},{8,12},{12,8},{9,1... | collective-permute-start | bytes 1824776 | tf_op jit(solution)/shard_map/ppermute | solution.py:114
  74.8 4.4 %copy-start.11 = (bf16[264,1152]{1,0:T(8,128)(2,1)}, bf16[264,1152]{1,0:T(8,128)(2,1)S(1)}, u32[]{:S(2)}) copy-start(bf16[264,1152]{1,0:T(8,128)(2,1)S(1)} %collective-permute-done.12.refs_14_) | copy-start | bytes 1824772
  74.8 15.7 %collective-permute-start.5 = (bf16[264,1024]{1,0:T(8,128)(2,1)S(1)}, bf16[264,1024]{1,0:T(8,128)(2,1)S(1)}, u32[]{:S(2)}, u32[]{:S(2)}) collective-permute-start(bf16[264,1024]{1,0:T(8,128)(2,1)S(1)} %collective-permute-done.3.refs_4_), channel_id=1, source_target_pairs={{0,56},{8,0},{16,8},{24,16},{32,24},{40,32},{48,40},{56,48},{1,57}... | collective-permute-start | bytes 1622024 | tf_op jit(solution)/shard_map/ppermute | solution.py:125
  77.0 2.3 copy-start.12
  77.0 28.3 %collective-permute-start.14 = (bf16[264,1152]{1,0:T(8,128)(2,1)S(1)}, bf16[264,1152]{1,0:T(8,128)(2,1)S(1)}, u32[]{:S(2)}, u32[]{:S(2)}) collective-permute-start(bf16[264,1152]{1,0:T(8,128)(2,1)S(1)} %collective-permute-done.13.refs_15_), channel_id=1, source_target_pairs={{0,4},{4,0},{1,5},{5,1},{2,6},{6,2},{3,7},{7,3},{8,12},{12,8},{9,1... | collective-permute-start | bytes 1824776 | tf_op jit(solution)/shard_map/ppermute | solution.py:114
  79.2 47.6 %copy-start.3 = (bf16[264,1152]{1,0:T(8,128)(2,1)}, bf16[264,1152]{1,0:T(8,128)(2,1)S(1)}, u32[]{:S(2)}) copy-start(bf16[264,1152]{1,0:T(8,128)(2,1)S(1)} %collective-permute-done.19.refs_21_) | copy-start | bytes 1824772
  79.3 16.7 %collective-permute-start.4 = (bf16[264,1024]{1,0:T(8,128)(2,1)S(1)}, bf16[264,1024]{1,0:T(8,128)(2,1)S(1)}, u32[]{:S(2)}, u32[]{:S(2)}) collective-permute-start(bf16[264,1024]{1,0:T(8,128)(2,1)S(1)} %collective-permute-done.2.refs_3_), channel_id=1, source_target_pairs={{0,8},{8,16},{16,24},{24,32},{32,40},{40,48},{48,56},{56,0},{1,9},... | collective-permute-start | bytes 1622024 | tf_op jit(solution)/shard_map/ppermute | solution.py:124
  90.5 36.4 %copy-start.4 = (bf16[264,1024]{1,0:T(8,128)(2,1)}, bf16[264,1024]{1,0:T(8,128)(2,1)S(1)}, u32[]{:S(2)}) copy-start(bf16[264,1024]{1,0:T(8,128)(2,1)S(1)} %collective-permute-done.5.refs_6_) | copy-start | bytes 1622020
  90.5 16.8 %collective-permute-start.23 = (bf16[136,1152]{1,0:T(8,128)(2,1)S(1)}, bf16[136,1152]{1,0:T(8,128)(2,1)S(1)}, u32[]{:S(2)}, u32[]{:S(2)}) collective-permute-start(bf16[136,1152]{1,0:T(8,128)(2,1)S(1)} %slice.19), channel_id=1, source_target_pairs={{0,448},{64,0},{128,64},{192,128},{256,192},{320,256},{384,320},{4... | collective-permute-start | bytes 940040 | tf_op jit(solution)/shard_map/ppermute | solution.py:132
  96.0 20.6 %copy-start.5 = (bf16[264,1024]{1,0:T(8,128)(2,1)}, bf16[264,1024]{1,0:T(8,128)(2,1)S(1)}, u32[]{:S(2)}) copy-start(bf16[264,1024]{1,0:T(8,128)(2,1)S(1)} %collective-permute-done.4.refs_5_) | copy-start | bytes 1622020
  96.0 30.8 %collective-permute-start.20 = (bf16[264,1152]{1,0:T(8,128)(2,1)S(1)}, bf16[264,1152]{1,0:T(8,128)(2,1)}, u32[]{:S(2)}, u32[]{:S(2)}) collective-permute-start(bf16[264,1152]{1,0:T(8,128)(2,1)S(1)} %collective-permute-done.19.refs_21_), channel_id=1, source_target_pairs={{0,4},{4,0},{1,5},{5,1},{2,6},{6,2},{3,7},{7,3},{8,12},{12,8},{9,1... | collective-permute-start | bytes 1824776 | tf_op jit(solution)/shard_map/ppermute | solution.py:114
  99.0 27.9 %collective-permute-start.18 = (bf16[264,1152]{1,0:T(8,128)(2,1)}, bf16[264,1152]{1,0:T(8,128)(2,1)}, u32[]{:S(2)}, u32[]{:S(2)}) collective-permute-start(bf16[264,1152]{1,0:T(8,128)(2,1)} %collective-permute-done.17.refs_19_), channel_id=1, source_target_pairs={{0,4},{4,0},{1,5},{5,1},{2,6},{6,2},{3,7},{7,3},{8,12},{12,8},{9,1... | collective-permute-start | bytes 1824776 | tf_op jit(solution)/shard_map/ppermute | solution.py:114
  101.9 14.6 %copy-start.13 = (bf16[264,1152]{1,0:T(8,128)(2,1)}, bf16[264,1152]{1,0:T(8,128)(2,1)S(1)}, u32[]{:S(2)}) copy-start(bf16[264,1152]{1,0:T(8,128)(2,1)S(1)} %collective-permute-done.16.refs_18_) | copy-start | bytes 1824772
  101.9 11.3 %collective-permute-start.21 = (bf16[128,1152]{1,0:T(8,128)(2,1)S(1)}, bf16[128,1152]{1,0:T(8,128)(2,1)}, u32[]{:S(2)}, u32[]{:S(2)}) collective-permute-start(bf16[128,1152]{1,0:T(8,128)(2,1)S(1)} %slice.18), channel_id=1, source_target_pairs={{0,64},{64,128},{128,192},{192,256},{256,320},{320,384},{384,448},... | collective-permute-start | bytes 884744 | tf_op jit(solution)/shard_map/ppermute | solution.py:131
  105.3 11.2 %copy-start.14 = (bf16[264,1152]{1,0:T(8,128)(2,1)}, bf16[264,1152]{1,0:T(8,128)(2,1)S(1)}, u32[]{:S(2)}) copy-start(bf16[264,1152]{1,0:T(8,128)(2,1)S(1)} %collective-permute-done.14.refs_16_) | copy-start | bytes 1824772
  105.3 11.2 %collective-permute-start.6 = (bf16[128,1024]{1,0:T(8,128)(2,1)S(1)}, bf16[128,1024]{1,0:T(8,128)(2,1)S(1)}, u32[]{:S(2)}, u32[]{:S(2)}) collective-permute-start(bf16[128,1024]{1,0:T(8,128)(2,1)S(1)} %slice.16), channel_id=1, source_target_pairs={{0,8},{8,16},{16,24},{24,32},{32,40},{40,48},{48,56},{56,0},{1,9},... | collective-permute-start | bytes 786440 | tf_op jit(solution)/shard_map/ppermute | solution.py:133
  107.3 19.6 %copy-start.19 = (bf16[136,1152]{1,0:T(8,128)(2,1)}, bf16[136,1152]{1,0:T(8,128)(2,1)S(1)}, u32[]{:S(2)}) copy-start(bf16[136,1152]{1,0:T(8,128)(2,1)S(1)} %collective-permute-done.23.refs_25_) | copy-start | bytes 940036
  107.3 19.6 %collective-permute-start.24 = (bf16[136,1152]{1,0:T(8,128)(2,1)S(1)}, bf16[136,1152]{1,0:T(8,128)(2,1)}, u32[]{:S(2)}, u32[]{:S(2)}) collective-permute-start(bf16[136,1152]{1,0:T(8,128)(2,1)S(1)} %collective-permute-done.23.refs_25_), channel_id=1, source_target_pairs={{0,4},{4,0},{1,5},{5,1},{2,6},{6,2},{3,7},{7,3},{8,12},{12,8},{9,1... | collective-permute-start | bytes 940040 | tf_op jit(solution)/shard_map/ppermute | solution.py:114
  113.2 13.6 %collective-permute-start.22 = (bf16[128,1152]{1,0:T(8,128)(2,1)}, bf16[128,1152]{1,0:T(8,128)(2,1)}, u32[]{:S(2)}, u32[]{:S(2)}) collective-permute-start(bf16[128,1152]{1,0:T(8,128)(2,1)} %collective-permute-done.21.refs_23_), channel_id=1, source_target_pairs={{0,4},{4,0},{1,5},{5,1},{2,6},{6,2},{3,7},{7,3},{8,12},{12,8},{9,1... | collective-permute-start | bytes 884744 | tf_op jit(solution)/shard_map/ppermute | solution.py:114
  116.6 0.7 copy-start.20
  117.3 9.6 %collective-permute-start.7 = (bf16[136,1024]{1,0:T(8,128)(2,1)S(1)}, bf16[136,1024]{1,0:T(8,128)(2,1)}, u32[]{:S(2)}, u32[]{:S(2)}) collective-permute-start(bf16[136,1024]{1,0:T(8,128)(2,1)S(1)} %slice.17), channel_id=1, source_target_pairs={{0,56},{8,0},{16,8},{24,16},{32,24},{40,32},{48,40},{56,48},{1,57}... | collective-permute-start | bytes 835592 | tf_op jit(solution)/shard_map/ppermute | solution.py:134
  166.0 6.2 %collective-permute-start.25 = (f32[1,4096]{1,0:T(1,128)}, f32[1,4096]{1,0:T(1,128)S(1)}, u32[]{:S(2)}, u32[]{:S(2)}) collective-permute-start(f32[1,4096]{1,0:T(1,128)} %get-tuple-element.10), channel_id=1, source_target_pairs={{0,2},{2,0},{1,3},{3,1},{4,6},{6,4},{5,7},{7,5},{8,10},{10,8},{9,1... | collective-permute-start | bytes 49160 | tf_op jit(solution)/shard_map/ppermute | solution.py:353
  202.9 20.9 %all-to-all-start.1 = ((bf16[16,128,128]{2,1,0:T(8,128)(2,1)}), bf16[16,128,128]{2,1,0:T(8,128)(2,1)S(1)}, u32[]{:S(2)}, u32[]{:S(2)}) async-start(bf16[16,128,128]{2,1,0:T(8,128)(2,1)} %bitcast.10), calls=%async_computation.1 | async-start | bytes 1048576 | tf_op jit(solution)/shard_map/all_to_all | solution.py:361
  377.7 14.5 %all-to-all-start.7 = ((f32[4,128,128]{2,1,0:T(8,128)}), f32[4,128,128]{2,1,0:T(8,128)S(1)}, u32[]{:S(2)}, u32[]{:S(2)}) async-start(f32[4,128,128]{2,1,0:T(8,128)} %broadcast_in_dim.26), calls=%async_computation.7 | async-start | bytes 524288 | tf_op jit(solution)/shard_map/all_to_all | solution.py:25
